TPU v7x, 128 devices: a whole 4x4x4 slice. The times are simulated.
128 devices in a mesh: seq: 8 (over x, y_hi), fsdp: 16 (over z, y_lo, core).
Axes of the slice: x: 4, y: 4 (y_hi: 2, y_lo: 2; y = y_hi * 2 + y_lo), z: 4, core: 2. Of those that a mesh axis runs over, the one named last changes fastest.
Arguments:
- tokens: bfloat16 [16, 1024, 8192], P('fsdp', 'seq'), may hold values from -6 to 6
- norm_gain: float32 [8192], replicated, may hold values from 0.3 to 3
- w_query: bfloat16 [8192, 4096], P(('seq', 'fsdp')), may hold values from -1 to 1
- key_weight: bfloat16 [8192, 512], P(('seq', 'fsdp')), may hold values from -1 to 1
- value_weight: bfloat16 [8192, 512], P(('seq', 'fsdp')), may hold values from -0.0625 to 0.0625
- w_out: bfloat16 [4096, 8192], P(None, ('seq', 'fsdp')), may hold values from -0.09375 to 0.09375
Outputs:
- result: float32 [16, 1024, 8192], P('fsdp', 'seq')
All inputs are finite; a program needn't handle non-finite values.
Results may differ from a plain program's by a relative error of at most 0.04.
Values may be sent and summed in bfloat16 or wider, within the bound.
A program may use at most 128 MiB of HBM per device.

v0:
```python
import jax
import jax.numpy as jnp
from jax import lax
from jax.sharding import PartitionSpec as P

HEAD_SIZE = 128


def in_one_piece(arrays, axis, dim, along):
    widths = [a.shape[along] for a in arrays]
    both = jnp.concatenate(arrays, axis=along)
    filled = lax.all_gather(both, axis, axis=dim, tiled=True)
    return tuple(jnp.split(filled, [sum(widths[:k]) for k in range(1, len(widths))], axis=along))


def in_blocks(array, dim, peers):
    lengths = array.shape
    blocks = array.reshape(*lengths[:dim], peers, lengths[dim] // peers, *lengths[dim + 1 :])
    return jnp.moveaxis(blocks, dim, 0)


def sum_at_owner(array, axis, dim):
    blocks = in_blocks(array, dim, lax.axis_size(axis))
    arrived = lax.all_to_all(blocks, axis, split_axis=0, concat_axis=0, tiled=True)
    return arrived.astype(jnp.float32).sum(axis=0)


def in_one_piece_2(arrays, axis, dim, along):
    both = jnp.concatenate(arrays, axis=along)
    filled, at, finished = (sum_at_owner(both, axis, dim), 0, [])
    for a in arrays:
        finished.append(lax.slice_in_dim(filled, at, at + a.shape[along], axis=along))
        at += a.shape[along]
    return tuple(finished)


def body(tokens, norm_gain, w_query, key_weight, value_weight, w_out):
    floats = tokens[0].astype(jnp.float32)
    mean_square = jnp.mean(floats * floats, axis=-1, keepdims=True)
    normed_input = (floats * lax.rsqrt(mean_square + 1e-05) * norm_gain).astype(jnp.bfloat16)
    spread = lax.all_to_all(normed_input[None], "seq", split_axis=2, concat_axis=1, tiled=True)[0]
    seq_length = spread.shape[0]
    group_size = lax.axis_size("seq")
    query_heads = w_query.shape[1] // HEAD_SIZE
    key_heads = key_weight.shape[1] // HEAD_SIZE
    group_width = query_heads // key_heads
    local_heads = query_heads // group_size
    copies = group_width // local_heads
    portions = in_one_piece((w_query, key_weight, value_weight), "fsdp", 0, 1)
    query_part, key_part, value_part = tuple(
        (jnp.dot(spread, portion, preferred_element_type=jnp.float32) for portion in portions)
    )
    key_wide = jnp.repeat(
        key_part.reshape(seq_length, key_heads, HEAD_SIZE), copies, axis=1
    ).reshape(seq_length, group_size * HEAD_SIZE)
    value_wide = jnp.repeat(
        value_part.reshape(seq_length, key_heads, HEAD_SIZE), copies, axis=1
    ).reshape(seq_length, group_size * HEAD_SIZE)
    query_sum, key_sum, value_sum = (
        sum_at_owner(query_part.astype(jnp.bfloat16), "seq", 1),
        *in_one_piece_2(
            (key_wide.astype(jnp.bfloat16), value_wide.astype(jnp.bfloat16)), "seq", 1, 0
        ),
    )
    key_rows = key_sum.astype(jnp.bfloat16)
    value_rows = value_sum.astype(jnp.bfloat16)
    queries = jnp.transpose(
        query_sum.astype(jnp.bfloat16).reshape(seq_length, local_heads, HEAD_SIZE), (1, 0, 2)
    )
    scale = HEAD_SIZE ** (-0.5)
    row_ids = lax.broadcasted_iota(jnp.int32, (seq_length, seq_length), 0)
    col_ids = lax.broadcasted_iota(jnp.int32, (seq_length, seq_length), 1)
    causal = row_ids >= col_ids

    def one_head(query_head):
        scores = (
            jnp.einsum("qd,kd->qk", query_head, key_rows, preferred_element_type=jnp.float32)
            * scale
        )
        scores = jnp.where(causal, scores, jnp.float32(-1e30))
        top = jnp.max(scores, axis=-1, keepdims=True)
        weights = jnp.exp(scores - top)
        probs = (weights / jnp.sum(weights, axis=-1, keepdims=True)).astype(jnp.bfloat16)
        return jnp.dot(probs, value_rows, preferred_element_type=jnp.float32).astype(jnp.bfloat16)

    attended = lax.map(one_head, queries)
    heads_out = jnp.transpose(attended, (1, 0, 2)).reshape(seq_length, local_heads * HEAD_SIZE)
    out_columns = lax.all_gather(w_out, "fsdp", axis=1, tiled=True)
    mixed = jnp.dot(
        lax.all_gather(heads_out, "seq", axis=1, tiled=True),
        out_columns,
        preferred_element_type=jnp.float32,
    )
    branch = mixed.astype(jnp.bfloat16)
    returned = lax.all_to_all(branch[None], "seq", split_axis=1, concat_axis=2, tiled=True)
    return tokens.astype(jnp.float32) + returned.astype(jnp.float32)


def solution(mesh):
    placed = (
        P("fsdp", "seq", None),
        P(),
        P(("seq", "fsdp"), None),
        P(("seq", "fsdp"), None),
        P(("seq", "fsdp"), None),
        P(None, ("seq", "fsdp")),
    )
    return jax.shard_map(
        body, mesh=mesh, in_specs=placed, out_specs=P("fsdp", "seq", None), check_vma=False
    )
```

profile of v0, /device:TPU:1, one launch (start us, length us, event | category | flops | bytes accessed | tf_op | source)
XLA Modules:
  0.0 554.2 jit_solution(15697988389426904720)
XLA Ops:
  6.5 2.2 pad_maximum_fusion
  10.8 2.6 fusion.20
  13.5 9.5 %copy.45 = bf16[1,128,8192]{1,0,2:T(2,128)(2,1)} copy(bf16[1,128,8192]{2,1,0:T(8,128)(2,1)} %fusion.20) | data formatting | bytes 4194304 | tf_op jit(solution)/shard_map/convert_element_type | solution.py:40
  23.6 46.5 %reduce.3 = bf16[8192,128]{1,0:T(8,128)(2,1)} reduce(bf16[8192,1,128]{2,1,0:T(2,128)(2,1)} %bitcast.70, bf16[]{:T(256)} %broadcast.35), dimensions={1}, to_apply=%bitcast.41.reduce_sub_computation | reduce | bytes 4194306
  70.1 5.8 %reshape.69 = bf16[8,2,65536]{2,1,0:T(2,128)(2,1)} reshape(bf16[8192,128]{1,0:T(8,128)(2,1)} %reduce.3) | data formatting | bytes 4194304
  75.9 34.2 %all_to_all.34 = bf16[8,2,65536]{2,1,0:T(2,128)(2,1)} all-to-all(bf16[8,2,65536]{2,1,0:T(2,128)(2,1)} %reshape.69), channel_id=1, replica_groups=mesh['seq'=8,'fsdp'=16] {'seq'}, dimensions={0} | all-to-all | bytes 4194304 | tf_op jit(solution)/shard_map/all_to_all | solution.py:41
  110.1 6.7 %reshape.70 = bf16[8192,1,128]{2,1,0:T(2,128)(2,1)} reshape(bf16[8,2,65536]{2,1,0:T(2,128)(2,1)} %all_to_all.34) | data formatting | bytes 4194304
  116.8 3.8 copy.59
  120.6 3.9 copy.46
  124.5 2.7 slice_bitcast_fusion.1
  127.2 2.3 copy.51
  130.7 3.3 convolution_convert_fusion
  135.9 2.3 maximum_bitcast_fusion
  138.2 4.6 all-to-all-start.2
  143.5 14.8 %fusion.15 = bf16[1024,4096]{1,0:T(8,128)(2,1)} fusion(bf16[1024,1024]{1,0:T(8,128)(2,1)} %bitcast.80, bf16[1024,5120]{1,0:T(8,128)(2,1)} %all-gather.4.cloned.1.call-done), kind=kOutput, calls=%fused_computation.20 | convolution fusion | flops 8594128896 | bytes 18874368 | tf_op jit(solution)/shard_map/dot_general | solution.py:51
  158.3 7.7 %copy.67 = bf16[128,8,8,512]{3,2,0,1:T(8,128)(2,1)} copy(bf16[128,8,8,512]{3,2,1,0:T(8,128)(2,1)} %bitcast.76) | data formatting | bytes 16777216 | tf_op jit(solution)/shard_map/reshape | solution.py:18
  166.0 35.0 %all-to-all-done.2 = bf16[8,2048,128]{2,1,0:T(8,128)(2,1)} async-done(((bf16[8,2048,128]{2,1,0:T(8,128)(2,1)}), bf16[8,2048,128]{2,1,0:T(8,128)(2,1)}, u32[]{:S(2)}, u32[]{:S(2)}) %all-to-all-start.2) | async-done | bytes 4194336 | tf_op jit(solution)/shard_map/all_to_all | solution.py:24
  201.0 6.0 %all-to-all-start.1 = ((bf16[8,1024,512]{2,1,0:T(8,128)(2,1)}), bf16[8,1024,512]{2,1,0:T(8,128)(2,1)}, u32[]{:S(2)}, u32[]{:S(2)}) async-start(bf16[8,1024,512]{2,1,0:T(8,128)(2,1)} %bitcast.69), calls=%async_computation.1 | async-start | bytes 16777216 | tf_op jit(solution)/shard_map/all_to_all | solution.py:24
  207.1 3.1 reduce.2
  211.0 111.2 %all-to-all-done.1 = bf16[8,1024,512]{2,1,0:T(8,128)(2,1)} async-done(((bf16[8,1024,512]{2,1,0:T(8,128)(2,1)}), bf16[8,1024,512]{2,1,0:T(8,128)(2,1)}, u32[]{:S(2)}, u32[]{:S(2)}) %all-to-all-start.1) | async-done | bytes 8388640 | tf_op jit(solution)/shard_map/all_to_all | solution.py:24
  322.1 5.2 reduce_sum.40
  328.9 15.9 %while.11 = (s32[]{:T(128)}, bf16[4,1024,128]{1,2,0:T(8,128)(2,1)}, bf16[4,1024,128]{1,2,0:T(8,128)(2,1)}, bf16[1024,128]{1,0:T(8,128)(2,1)}, bf16[1024,128]{1,0:T(8,128)(2,1)S(1)}, /*index=5*/s32[]{:T(128)}) while((s32[]{:T(128)}, bf16[4,1024,128]{1,2,0:T(8,128)(2,1)}, bf16[4,1024,128]{1,2,0:T(8,128)(2,1)}, ...), condition=%wide.region_6.7_spmd.clone, body=%wide.region_3.6_spmd.clone.sunk | while | flops 552728576 | bytes 14701637 | solution.py:86
  344.8 109.3 %all-gather.6.cloned.1.call-done = bf16[1024,4096]{0,1:T(8,128)(2,1)} async-done(((bf16[1024,512]{0,1:T(8,128)(2,1)}), bf16[1024,4096]{0,1:T(8,128)(2,1)}) %all-gather.6.cloned.1.call-update) | async-done | bytes 8388624 | tf_op jit(solution)/shard_map/all_gather | solution.py:90
  454.1 13.8 %convert_bitcast_fusion = bf16[1,1024,1024]{2,1,0:T(8,128)(2,1)S(1)} fusion(bf16[1024,4096]{0,1:T(8,128)(2,1)} %all-gather.6.cloned.1.call-done, bf16[4096,1024]{0,1:T(8,128)(2,1)} %all-gather.8.cloned.1.call-done), kind=kOutput, calls=%fused_computation.29 | convolution fusion | flops 8590983168 | bytes 18874368 | tf_op jit(solution)/shard_map/dot_general | solution.py:89
  467.9 5.2 copy.69
  473.2 14.4 %reduce.4 = bf16[1024,1024]{1,0:T(8,128)(2,1)} reduce(bf16[1024,1,1024]{2,1,0:T(2,128)(2,1)} %bitcast.71, bf16[]{:T(256)} %broadcast.35), dimensions={1}, to_apply=%bitcast.60.reduce_sub_computation | reduce | bytes 4194306
  487.6 6.3 %reshape.71 = bf16[8,2,65536]{2,1,0:T(2,128)(2,1)} reshape(bf16[1024,1024]{1,0:T(8,128)(2,1)} %reduce.4) | data formatting | bytes 4194304
  493.8 30.9 %all_to_all.35 = bf16[8,2,65536]{2,1,0:T(2,128)(2,1)} all-to-all(bf16[8,2,65536]{2,1,0:T(2,128)(2,1)} %reshape.71), channel_id=1, replica_groups=mesh['seq'=8,'fsdp'=16] {'seq'}, dimensions={0} | all-to-all | bytes 4194304 | tf_op jit(solution)/shard_map/all_to_all | solution.py:95
  524.8 6.7 %reshape.72 = bf16[1024,1,1024]{2,1,0:T(2,128)(2,1)} reshape(bf16[8,2,65536]{2,1,0:T(2,128)(2,1)} %all_to_all.35) | data formatting | bytes 4194304
  531.5 6.5 %copy.68 = f32[1,8,128,1024]{3,1,2,0:T(8,128)} copy(bf16[1,8,128,1024]{3,0,2,1:T(2,128)(2,1)} %bitcast.73) | data formatting | bytes 6291456 | tf_op jit(solution)/shard_map/convert_element_type | solution.py:96
  538.1 4.9 reshape.66
  543.0 4.6 convert_add_fusion
  (44 shorter events, 24.7 us)
Async XLA Ops:
  6.5 4.3 copy-start
  6.5 118.0 %all-gather.4.cloned.1.call-start = ((), (), s32[]{:S(2)}) async-start(), calls=%async_computation.4 | async-start | bytes 11141120 | tf_op jit(solution)/shard_map/all_gather | solution.py:12
  130.7 3.3 copy-start.1
  130.7 3.3 copy-start.2
  138.2 62.8 %all-to-all-start.2 = ((bf16[8,2048,128]{2,1,0:T(8,128)(2,1)}), bf16[8,2048,128]{2,1,0:T(8,128)(2,1)}, u32[]{:S(2)}, u32[]{:S(2)}) async-start(bf16[8,2048,128]{2,1,0:T(8,128)(2,1)} %maximum_bitcast_fusion), calls=%async_computation.2 | async-start | bytes 8388608 | tf_op jit(solution)/shard_map/all_to_all | solution.py:24
  142.8 202.1 %all-gather.8.cloned.1.call-start = ((), (), s32[]{:S(2)}) async-start(), calls=%async_computation.6 | async-start | bytes 8912896 | tf_op jit(solution)/shard_map/all_gather | solution.py:88
  201.0 121.1 %all-to-all-start.1 = ((bf16[8,1024,512]{2,1,0:T(8,128)(2,1)}), bf16[8,1024,512]{2,1,0:T(8,128)(2,1)}, u32[]{:S(2)}, u32[]{:S(2)}) async-start(bf16[8,1024,512]{2,1,0:T(8,128)(2,1)} %bitcast.69), calls=%async_computation.1 | async-start | bytes 16777216 | tf_op jit(solution)/shard_map/all_to_all | solution.py:24
  207.0 247.1 %all-gather.6.cloned.1.call-start = ((), (), s32[]{:S(2)}) async-start(), calls=%async_computation.5 | async-start | bytes 9437184 | tf_op jit(solution)/shard_map/all_gather | solution.py:90
Sparse Core Ops, SparseCore 0:
  9.0 65.5 all-gather.3
  145.3 172.0 all-gather.7
  344.9 109.1 all-gather.5
where the time goes:
time: 557 us; the launch traced here: 554 us
  waiting for transfers between devices  256 us (46%)
  other arithmetic  85.2 us (15%)
  local copies, waits for them, and re-layouts  80.4 us (14%)
  blocking collectives  65.1 us (12%)
  matrix products  43.3 us (8%)
  between operations  13.2 us (2%)
  starting transfers between devices  10.9 us (2%)
    all_to_all x2, waiting for transfers between devices, sum_at_owner(): lax.all_to_all(blocks, axis, split_axis=0, concat_axis=0, tiled=True)  146 us
    all_gather x1, waiting for transfers between devices, body(): lax.all_gather(heads_out, 'seq', axis=1, tiled=True)  109 us
    unnamed x2, other arithmetic  60.9 us
    all_to_all x1, blocking collectives, body(): lax.all_to_all(normed_input[None], 'seq', split_axis=2, concat_axis=1, ti...  34.2 us
    all_to_all x1, blocking collectives, body(): lax.all_to_all(branch[None], 'seq', split_axis=1, concat_axis=2, tiled=True)  30.9 us
    unnamed x12, local copies, waits for them, and re-layouts  29.9 us
    dot_general x3, matrix products, body(): jnp.dot(spread, portion, preferred_element_type=jnp.float32)  19.4 us
    dot_general x1, matrix products, body(): jnp.dot(lax.all_gather(heads_out, 'seq', axis=1, tiled=True), out_columns...  13.8 us
  transfers between devices with their start and end apart: 5, of which 3 were waited for; matrix products, arithmetic and copies ran while one was open for 24% of the time, Pallas kernels for 0%

commit v1 on v0

v1 whole, which is shorter than its diff:
```python
import jax
import jax.numpy as jnp
from jax import lax
from jax.experimental import pallas as pl
from jax.experimental.pallas import tpu as pltpu
from jax.sharding import PartitionSpec as P

HD = 128
BLK = 128
D = 8192
NQ = 1024
NKV = 256
NW = NQ + NKV
NO = 2048
MESH = pl.DeviceIdType.MESH
SLOT = (0, 1, 3, 2)


def kernel(
    tok, gain, wq, wk, wv, wot, out,
    W, WO, X, Q, KV, HG, OB, acc,
    loc, xs, xr, xss, xrs, wS, wR, wRD, oS, oR, oRD, kvs, kvr, hs, hr, os_, or_, ol,
):
    sx = lax.axis_index("seq")
    f = lax.axis_index("fsdp")
    x, yh = sx // 2, sx % 2
    z, yl, c = f // 4, (f // 2) % 2, f % 2
    y = 2 * yh + yl
    p = yh * 16 + f

    def dev(xx, yy, zz, cc):
        return (2 * xx + yy // 2, 4 * zz + 2 * (yy % 2) + cc)

    def at_x(r):
        return dev((x + r) % 4, y, z, c)

    sib = dev(x, y, z, 1 - c)
    pair = dev(x, (y + 2) % 4, z, c)

    barrier = pltpu.get_barrier_semaphore()
    peers = [at_x(1), at_x(2), at_x(3), sib, pair]
    peers += [dev(x, (y + 1) % 4, z, c), dev(x, (y + 3) % 4, z, c)]
    peers += [dev(x, y, (z + 1) % 4, c), dev(x, y, (z + 3) % 4, c)]
    for d in peers:
        pl.semaphore_signal(barrier, inc=1, device_id=d, device_id_type=MESH)

    def own_parts(xx, row):
        cq = pl.ds(pl.multiple_of(xx * NQ, NQ), NQ)
        ck = pl.ds(pl.multiple_of(xx * HD, HD), HD)
        return (
            (wq.at[:, cq], W.at[row, p, :, 0:NQ]),
            (wk.at[:, ck], W.at[row, p, :, NQ : NQ + HD]),
            (wv.at[:, ck], W.at[row, p, :, NQ + HD : NW]),
        )

    tok_in = pltpu.make_async_copy(tok, X.at[0], loc.at[0])
    tok_in.start()
    wo_in = pltpu.make_async_copy(wot, WO.at[p], loc.at[1])
    wo_in.start()
    w_in = [
        pltpu.make_async_copy(s, d, loc.at[2 + k])
        for k, (s, d) in enumerate(own_parts(x, x))
    ]
    for cp in w_in:
        cp.start()

    pl.semaphore_wait(barrier, len(peers))

    xsends = []
    for r in (1, 3, 2):
        for k, (s, d) in enumerate(own_parts((x + r) % 4, x)):
            cp = pltpu.make_async_remote_copy(
                s, d, xs.at[r, k], xr.at[4 - r, k], device_id=at_x(r), device_id_type=MESH
            )
            cp.start()
            xsends.append(cp)

    def gather(buf, S, R, RD, is_w):
        def piece(h, pp):
            return buf.at[h, pp] if is_w else buf.at[pp, h]

        def coords(h, a1, a2):
            g, sg = h // 2, 1 - 2 * (h % 2)
            yy = (y + 4 + sg * (a1 * g + a2 * (1 - g))) % 4
            zz = (z + 4 + sg * (a1 * (1 - g) + a2 * g)) % 4
            return yy, zz

        def ref(h, u1, u2):
            yy, zz = coords(h, u1, u2)
            return piece(h, (yy // 2) * 16 + 4 * zz + 2 * (yy % 2) + c)

        def send(h, u1, u2, k):
            a1, a2 = ((1, 0), (-1, 0), (0, 1), (0, -1))[k]
            yy, zz = coords(h, a1, a2)
            r = ref(h, u1, u2)
            pltpu.make_async_remote_copy(
                r, r, S.at[k], R.at[h, (u1 - a1) % 4, (u2 - a2) % 4],
                device_id=dev(x, yy, zz, c), device_id_type=MESH,
            ).start()

        def across(h, u1, u2):
            r = ref(h, u1, u2)
            pltpu.make_async_remote_copy(
                r, r, S.at[4], RD, device_id=sib, device_id_type=MESH
            ).start()

        def recv(h, u1, u2):
            r = ref(h, u1, u2)
            pltpu.make_async_remote_copy(
                r, r, S.at[4], R.at[h, u1, u2], device_id=sib, device_id_type=MESH
            ).wait_recv()

        def over_pieces(steps):
            def one(h, _):
                for u1, u2, ks in steps:
                    if (u1, u2) != (0, 0):
                        recv(h, u1, u2)
                    for k in ks:
                        send(h, u1, u2, k)
                    across(h, u1, u2)
                return 0

            lax.fori_loop(0, 4, one, 0)

        def many(n):
            return buf.at[:, 0 : n // 4] if is_w else buf.at[0 : n // 4]

        def whole(sem, n):
            return pltpu.make_async_remote_copy(
                many(n), many(n), sem, sem, device_id=sib, device_id_type=MESH
            )

        def wave(n):
            if n == 0:
                over_pieces([(0, 0, (0, 1, 2, 3))])
            elif n == 1:
                over_pieces([(3, 0, (0, 2, 3)), (1, 0, (2, 3))])
            elif n == 2:
                over_pieces([(2, 0, (2, 3)), (0, 3, (2,))])
            elif n == 3:
                over_pieces([(3, 3, (2,)), (1, 3, (2,))])
            elif n == 4:
                over_pieces([(2, 3, (2,)), (0, 1, ()), (0, 2, ())])
            elif n == 5:
                over_pieces([(u, v, ()) for u in (3, 1, 2) for v in (1, 2)])

        def arrived():
            whole(RD, 64).wait_recv()

        def sent():
            for k, n in enumerate((8, 4, 32, 16, 64)):
                whole(S.at[k], n).wait_send()

        return wave, arrived, sent

    w_wave, w_arrived, w_sent = gather(W, wS, wR, wRD, True)
    o_wave, o_arrived, o_sent = gather(WO, oS, oR, oRD, False)

    tok_in.wait()

    def norm(r, _):
        rows = pl.ds(pl.multiple_of(r * 16, 16), 16)
        v = X[0, rows, :].astype(jnp.float32)
        ms = jnp.mean(v * v, axis=-1, keepdims=True)
        X[0, rows, :] = (v * lax.rsqrt(ms + 1e-05) * gain[...]).astype(jnp.bfloat16)
        return 0

    lax.fori_loop(0, BLK // 16, norm, 0)

    def x_piece(a, u, k, start):
        sg = 1 - 2 * a
        r = sg if k == 0 else -sg
        src = X.at[SLOT[(sg * u) % 4], 64 * a : 64 * a + 64]
        dst = X.at[SLOT[(sg * u - r) % 4], 64 * a : 64 * a + 64]
        cp = pltpu.make_async_remote_copy(
            src, dst, xss.at[a, 2 if u else k], xrs.at[a, (u - r * sg) % 4],
            device_id=at_x(r), device_id_type=MESH,
        )
        if start:
            cp.start()
        return cp

    def x_recv(a, u):
        sg = 1 - 2 * a
        d = X.at[SLOT[(sg * u) % 4], 64 * a : 64 * a + 64]
        pltpu.make_async_remote_copy(
            d, d, xss.at[a, 0], xrs.at[a, u], device_id=sib, device_id_type=MESH
        ).wait_recv()

    x_own = [x_piece(a, 0, k, True) for k in (0, 1) for a in (0, 1)]

    wo_in.wait()
    o_wave(0)

    for cp in w_in:
        cp.wait()
    for r in (1, 3, 2):
        for k, (s, d) in enumerate(own_parts((x + r) % 4, (x + r) % 4)):
            pltpu.make_async_remote_copy(
                d, d, xs.at[r, k], xr.at[r, k], device_id=sib, device_id_type=MESH
            ).wait_recv()
    w_wave(0)
    o_wave(1)
    w_wave(1)
    w_wave(2)
    x_fwd = []
    for a in (0, 1):
        x_recv(a, 3)
        x_fwd.append(x_piece(a, 3, 0, True))
    w_wave(3)
    w_wave(4)
    w_wave(5)
    o_wave(2)
    o_wave(3)
    w_arrived()
    for a in (0, 1):
        x_recv(a, 1)

    def project(lo, hi):
        m = (hi - lo) * BLK

        def step(kc, _):
            cols = pl.ds(pl.multiple_of(kc * 1024, 1024), 1024)
            xk = X[lo:hi, :, cols].reshape(m, 1024)
            wkc = W[kc // 2, pl.ds((kc % 2) * 16, 16)].reshape(1024, NW)
            d = jnp.dot(xk, wkc, preferred_element_type=jnp.float32)

            @pl.when(kc == 0)
            def _():
                acc[0:m, :] = d

            @pl.when(kc > 0)
            def _():
                acc[0:m, :] += d

            return 0

        lax.fori_loop(0, 8, step, 0)
        cps = []
        for s in range(lo, hi):
            off = SLOT.index(s)
            i = (x + off) % 4
            rows = slice((s - lo) * BLK, (s - lo + 1) * BLK)
            Q[i] = acc[rows, 0:NQ].astype(jnp.bfloat16)
            KV[2 * i + yh] = acc[rows, NQ:NW].astype(jnp.bfloat16)
            ref = KV.at[2 * i + yh]
            cp = pltpu.make_async_remote_copy(
                ref, ref, kvs.at[off], kvr.at[off], device_id=pair, device_id_type=MESH
            )
            cp.start()
            cps.append(cp)
        return cps

    kv_cps = project(0, 3)
    o_wave(4)
    for a in (0, 1):
        x_recv(a, 2)
    kv_cps += project(3, 4)
    for off in range(4):
        i = (x + off) % 4
        ref = KV.at[2 * i + 1 - yh]
        pltpu.make_async_remote_copy(
            ref, ref, kvs.at[off], kvr.at[off], device_id=pair, device_id_type=MESH
        ).wait_recv()
    o_wave(5)

    scale = HD ** (-0.5)

    def h_ref(j, a, u):
        sg = 1 - 2 * a
        return HG.at[j, (x + 4 + sg * u) % 4, 2 * a : 2 * a + 2]

    def h_send(j, a, u, k):
        sg = 1 - 2 * a
        r = 1 if k != 1 else -1
        ref = h_ref(j, a, u)
        pltpu.make_async_remote_copy(
            ref, ref, hs.at[k], hr.at[j, a, (u - r) % 4],
            device_id=at_x(r * sg), device_id_type=MESH,
        ).start()

    def h_recv(j, a, u):
        ref = h_ref(j, a, u)
        pltpu.make_async_remote_copy(
            ref, ref, hs.at[0], hr.at[j, a, u], device_id=sib, device_id_type=MESH
        ).wait_recv()

    def attend(j, _):
        rows = pl.ds(pl.multiple_of(j * 32, 32), 32)
        for i in range(4):
            nk = (2 * i + 2) * BLK
            q = jnp.concatenate(
                [Q[i, rows, h * HD : (h + 1) * HD] for h in range(8)], axis=0
            )
            kk = KV[0 : 2 * i + 2, :, 0:HD].reshape(nk, HD)
            vv = KV[0 : 2 * i + 2, :, HD:NKV].reshape(nk, HD)
            s = lax.dot_general(
                q, kk, (((1,), (1,)), ((), ())), preferred_element_type=jnp.float32
            ) * scale
            qpos = (2 * i + yh) * BLK + j * 32 + lax.broadcasted_iota(
                jnp.int32, (256, nk), 0
            ) % 32
            kpos = lax.broadcasted_iota(jnp.int32, (256, nk), 1)
            s = jnp.where(qpos >= kpos, s, jnp.float32(-1e30))
            e = jnp.exp(s - jnp.max(s, axis=-1, keepdims=True))
            pr = (e * (1.0 / jnp.sum(e, axis=-1, keepdims=True))).astype(jnp.bfloat16)
            o = jnp.dot(pr, vv, preferred_element_type=jnp.float32).astype(jnp.bfloat16)
            for h in range(8):
                HG[j, x, i, :, h * HD : (h + 1) * HD] = o[h * 32 : (h + 1) * 32]
        for k in (0, 1):
            for a in (0, 1):
                h_send(j, a, 0, k)
        return 0

    lax.fori_loop(0, 4, attend, 0)

    def forward(j, _):
        for a in (0, 1):
            h_recv(j, a, 3)
            h_send(j, a, 3, 2)
        return 0

    lax.fori_loop(0, 4, forward, 0)
    o_arrived()

    def out_ref(j, xx):
        return out.at[
            pl.ds(pl.multiple_of(j * 32, 32), 32), pl.ds(pl.multiple_of(xx * NO, NO), NO)
        ]

    def mix(j, _):
        for a in (0, 1):
            h_recv(j, a, 1)
            h_recv(j, a, 2)

        def tile(n, _):
            t = jnp.zeros((BLK, 512), jnp.float32)
            for s in range(4):
                wo = WO[pl.ds(n * 8, 8), :, :, s * NQ : (s + 1) * NQ].reshape(512, NQ)
                t += lax.dot_general(
                    HG[j, s].reshape(BLK, NQ), wo, (((1,), (1,)), ((), ())),
                    preferred_element_type=jnp.float32,
                )
            OB[j, :, :, pl.ds(pl.multiple_of(n * 512, 512), 512)] = t.astype(
                jnp.bfloat16
            ).reshape(4, 32, 512)
            return 0

        lax.fori_loop(0, 4, tile, 0)
        for r in (2, 1, 3):
            pltpu.make_async_remote_copy(
                OB.at[j, (x + r) % 4], out_ref(j, x), os_.at[r], or_.at[j, 4 - r],
                device_id=at_x(r), device_id_type=MESH,
            ).start()
        pltpu.make_async_copy(OB.at[j, x], out_ref(j, x), ol).start()
        return 0

    lax.fori_loop(0, 4, mix, 0)

    for cp in xsends + x_own + x_fwd + kv_cps:
        cp.wait_send()
    w_sent()
    o_sent()
    for k in range(3):
        pltpu.make_async_remote_copy(
            HG.at[0], HG.at[0], hs.at[k], hs.at[k], device_id=sib, device_id_type=MESH
        ).wait_send()
    for r in (1, 2, 3):
        pltpu.make_async_remote_copy(
            OB.at[0], OB.at[0], os_.at[r], os_.at[r], device_id=sib, device_id_type=MESH
        ).wait_send()
    pltpu.make_async_copy(OB.at[0], OB.at[0], ol).wait()

    def finish(j, _):
        for r in (1, 2, 3):
            d = out_ref(j, (x + r) % 4)
            pltpu.make_async_remote_copy(
                d, d, os_.at[r], or_.at[j, r], device_id=sib, device_id_type=MESH
            ).wait_recv()
        return 0

    lax.fori_loop(0, 4, finish, 0)


def body(tokens, norm_gain, w_query, key_weight, value_weight, w_out):
    hbm = pl.BlockSpec(memory_space=pltpu.HBM)
    vmem = pl.BlockSpec(memory_space=pltpu.VMEM)
    bf = jnp.bfloat16
    dma = pltpu.SemaphoreType.DMA
    wot = w_out.T.reshape(4, 16, 4096)
    branch = pl.pallas_call(
        kernel,
        out_shape=jax.ShapeDtypeStruct((BLK, D), bf),
        in_specs=[hbm, vmem, hbm, hbm, hbm, hbm],
        out_specs=hbm,
        scratch_shapes=[
            pltpu.VMEM((4, 32, 64, NW), bf),
            pltpu.VMEM((32, 4, 16, 4096), bf),
            pltpu.VMEM((4, BLK, D), bf),
            pltpu.VMEM((4, BLK, NQ), bf),
            pltpu.VMEM((8, BLK, NKV), bf),
            pltpu.VMEM((4, 4, 4, 32, NQ), bf),
            pltpu.VMEM((4, 4, 32, NO), bf),
            pltpu.VMEM((3 * BLK, NW), jnp.float32),
            dma((5,)), dma((4, 3)), dma((4, 3)), dma((2, 3)), dma((2, 4)),
            dma((5,)), dma((4, 4, 4)), dma(()),
            dma((5,)), dma((4, 4, 4)), dma(()),
            dma((4,)), dma((4,)), dma((3,)), dma((4, 2, 4)),
            dma((4,)), dma((4, 4)), dma(()),
        ],
        compiler_params=pltpu.CompilerParams(
            collective_id=0, has_side_effects=True, vmem_limit_bytes=67043328
        ),
        name="sublayer",
    )(tokens[0], norm_gain.reshape(1, D), w_query, key_weight, value_weight, wot)
    return tokens.astype(jnp.float32) + branch[None].astype(jnp.float32)


def solution(mesh):
    placed = (
        P("fsdp", "seq", None),
        P(),
        P(("seq", "fsdp"), None),
        P(("seq", "fsdp"), None),
        P(("seq", "fsdp"), None),
        P(None, ("seq", "fsdp")),
    )
    return jax.shard_map(
        body, mesh=mesh, in_specs=placed, out_specs=P("fsdp", "seq", None), check_vma=False
    )
```

time: 557 us -> 185 us (0.33)
  waiting for transfers between devices: 256 us -> 0 us
  Pallas kernels: 0 us -> 180 us
  other arithmetic: 85.2 us -> 4.76 us
  local copies, waits for them, and re-layouts: 80.4 us -> 0 us
  blocking collectives: 65.1 us -> 0 us
  matrix products: 43.3 us -> 0 us
  between operations: 13.2 us -> 0.01 us
  starting transfers between devices: 10.9 us -> 0 us
    pallas_call x0 -> x1, Pallas kernels: none -> 180 us  [body(): pl.pallas_call(kernel, out_shape=jax.ShapeDtypeStruct((BLK, D), bf), in_s...]
    all_to_all x2 -> x0, waiting for transfers between devices: 146 us -> none  [sum_at_owner(): lax.all_to_all(blocks, axis, split_axis=0, concat_axis=0, tiled=True)]
    all_gather x3 -> x0, waiting for transfers between devices: 109 us -> none  [the longest x1 109 us: body(): lax.all_gather(heads_out, 'seq', axis=1, tiled=True)]
    all_to_all x2 -> x0, blocking collectives: 65.1 us -> none  [the longest x1 34.2 us: body(): lax.all_to_all(normed_input[None], 'seq', split_axis=2, concat_axis=1, ti...]
    unnamed x2 -> x0, other arithmetic: 60.9 us -> none
    dot_general x12 -> x0, matrix products: 43.3 us -> none  [the longest x3 19.4 us: body(): jnp.dot(spread, portion, preferred_element_type=jnp.float32)]
    unnamed x12 -> x0, local copies, waits for them, and re-layouts: 29.9 us -> none
    convert_element_type x3 -> x0, local copies, waits for them, and re-layouts: 21 us -> none  [the longest x2 11.5 us: body(): return tokens.astype(jnp.float32) + returned.astype(jnp.float32)]
  transfers between devices with their start and end apart: 5 -> 0, of which waited for: 3 -> 0; matrix products, arithmetic and copies ran while one was open for 24% -> 0% of each run, Pallas kernels for 0% -> 0%
where the time goes in v1:
time: 185 us
  Pallas kernels  180 us (97%)
  other arithmetic  4.76 us (3%)
    pallas_call x1, Pallas kernels, body(): pl.pallas_call(kernel, out_shape=jax.ShapeDtypeStruct((BLK, D), bf), in_s...  180 us
    add x1, other arithmetic, body(): return tokens.astype(jnp.float32) + branch[None].astype(jnp.float32)  4.76 us

profile of v1, /device:TPU:1, one launch (start us, length us, event | category | flops | bytes accessed | tf_op | source)
XLA Modules:
  0.0 184.7 jit_solution(8915025585832621902)
XLA Ops:
  0.0 179.9 %sublayer.1 = bf16[128,8192]{1,0:T(8,128)(2,1)} custom-call(bf16[128,8192]{1,0:T(8,128)(2,1)} %bitcast.8, f32[1,8192]{1,0:T(1,128)} %bitcast.10, bf16[64,4096]{1,0:T(8,128)(2,1)} %wq.1, bf16[64,512]{1,0:T(8,128)(2,1)} %wk.1, bf16[64,512]{1,0:T(8,128)(2,1)} %wv.1, bf16[4,16,4096]{2,1,0:T(8,128)(2,1)} %bitcast.9), custom_call_target="tpu_custom_call" | custom-call | tf_op jit(solution)/shard_map/sublayer/pallas_call | solution.py:391
  180.0 4.8 %convert_add_fusion = f32[1,128,8192]{2,1,0:T(8,128)} fusion(bf16[1,128,8192]{2,1,0:T(8,128)(2,1)} %param.6, bf16[128,8192]{1,0:T(8,128)(2,1)} %sublayer.1), kind=kLoop, calls=%fused_computation | loop fusion | flops 3145728 | bytes 8388608 | tf_op jit(solution)/shard_map/add | solution.py:416

commit v2 on v1

v2 whole, which is shorter than its diff:
```python
import jax
import jax.numpy as jnp
from jax import lax
from jax.experimental import pallas as pl
from jax.experimental.pallas import tpu as pltpu
from jax.sharding import PartitionSpec as P

HD = 128
BLK = 128
D = 8192
NQ = 1024
NKV = 256
NW = NQ + NKV
NO = 2048
MESH = pl.DeviceIdType.MESH
SLOT = (0, 1, 3, 2)
NX = 4


def kernel(
    tok, gain, wq, wk, wv, wot, out,
    W, WO, X, Q, KV, HG, OB, acc,
    T, loc, xs, xr, xss, xrs, wS, wR, wRD, oS, oR, oRD, kvs, kvr, hs, hr, os_, or_, ol,
):
    sx = lax.axis_index("seq")
    f = lax.axis_index("fsdp")
    x, yh = sx // 2, sx % 2
    z, yl, c = f // 4, (f // 2) % 2, f % 2
    y = 2 * yh + yl
    p = yh * 16 + f

    def dev(xx, yy, zz, cc):
        return (2 * xx + yy // 2, 4 * zz + 2 * (yy % 2) + cc)

    def at_x(r):
        return dev((x + r) % 4, y, z, c)

    sib = dev(x, y, z, 1 - c)
    pair = dev(x, (y + 2) % 4, z, c)

    barrier = pltpu.get_barrier_semaphore()
    peers = [at_x(1), at_x(2), at_x(3), sib, pair]
    peers += [dev(x, (y + 1) % 4, z, c), dev(x, (y + 3) % 4, z, c)]
    peers += [dev(x, y, (z + 1) % 4, c), dev(x, y, (z + 3) % 4, c)]
    for d in peers:
        pl.semaphore_signal(barrier, inc=1, device_id=d, device_id_type=MESH)

    def w_parts(xx, h):
        cq = pl.ds(pl.multiple_of(xx * NQ, NQ), NQ)
        ck = pl.ds(pl.multiple_of(xx * HD, HD), HD)
        return [
            (src.at[:, cc], W.at[h, yh, z, yl, c, :, lo:hi])
            for src, cc, lo, hi in (
                (wq, cq, 0, NQ), (wk, ck, NQ, NQ + HD), (wv, ck, NQ + HD, NW)
            )
        ]

    w_in = [
        pltpu.make_async_copy(s, d, loc.at[2 + k])
        for k, (s, d) in enumerate(w_parts(x, 0))
    ]
    for cp in w_in:
        cp.start()
    khalf = pl.ds(pl.multiple_of(c * 2048, 2048), 2048)
    other = pl.ds(pl.multiple_of((1 - c) * 2048, 2048), 2048)
    tok_in = pltpu.make_async_copy(tok, X.at[0], loc.at[0])
    tok_in.start()
    wo_in = pltpu.make_async_copy(wot.at[:, khalf], T.at[c], loc.at[1])
    wo_in.start()

    with jax.named_scope('p01_barrier'):
        pl.semaphore_wait(barrier, len(peers))

    xsends = []
    for r in (1, 3, 2):
        for k, (s, d) in enumerate(w_parts((x + r) % 4, 4 - r)):
            cp = pltpu.make_async_remote_copy(
                s, d, xs.at[r, k], xr.at[4 - r, k], device_id=at_x(r), device_id_type=MESH
            )
            cp.start()
            xsends.append(cp)
    wo_swap = pltpu.make_async_remote_copy(
        wot.at[:, other], T.at[c], loc.at[8], loc.at[9], device_id=sib, device_id_type=MESH
    )
    wo_swap.start()

    def w_got(r):
        for k, (s, d) in enumerate(w_parts(x, r)):
            pltpu.make_async_remote_copy(
                d, d, xs.at[r, k], xr.at[r, k], device_id=sib, device_id_type=MESH
            ).wait_recv()

    def gather(S, R, RD, piece, many):
        def coords(h, a1, a2):
            g, sg = h // 2, 1 - 2 * (h % 2)
            yy = (y + 4 + sg * (a1 * g + a2 * (1 - g))) % 4
            zz = (z + 4 + sg * (a1 * (1 - g) + a2 * g)) % 4
            return yy, zz

        def ref(h, u1, u2):
            yy, zz = coords(h, u1, u2)
            return piece(h, yy, zz)

        def send(h, u1, u2, k):
            a1, a2 = ((1, 0), (-1, 0), (0, 1), (0, -1))[k]
            yy, zz = coords(h, a1, a2)
            r = ref(h, u1, u2)
            pltpu.make_async_remote_copy(
                r, r, S.at[k], R.at[h, (u1 - a1) % 4, (u2 - a2) % 4],
                device_id=dev(x, yy, zz, c), device_id_type=MESH,
            ).start()

        def across(h, u1, u2):
            r = ref(h, u1, u2)
            pltpu.make_async_remote_copy(
                r, r, S.at[4], RD.at[int(u2 in (1, 2))], device_id=sib, device_id_type=MESH
            ).start()

        def recv(h, u1, u2):
            r = ref(h, u1, u2)
            pltpu.make_async_remote_copy(
                r, r, S.at[4], R.at[h, u1, u2], device_id=sib, device_id_type=MESH
            ).wait_recv()

        def over_pieces(steps, first=0, last=4, d2d=True):
            def one(h, _):
                for u1, u2, ks in steps:
                    if (u1, u2) != (0, 0):
                        recv(h, u1, u2)
                    for k in ks:
                        send(h, u1, u2, k)
                    if d2d:
                        across(h, u1, u2)
                return 0

            lax.fori_loop(first, last, one, 0)

        def whole(sem, n):
            return pltpu.make_async_remote_copy(
                many(n), many(n), sem, sem, device_id=sib, device_id_type=MESH
            )

        def wave(n):
            if n == 1:
                over_pieces([(3, 0, (0, 2, 3)), (1, 0, (2, 3))])
            elif n == 2:
                over_pieces([(2, 0, (2, 3)), (0, 3, (2,))])
            elif n == 3:
                over_pieces([(3, 3, (2,)), (1, 3, (2,))])
            elif n == 4:
                over_pieces([(2, 3, (2,))])
            elif n == 5:
                over_pieces([(u, 1, ()) for u in (0, 3, 1, 2)])
            elif n == 6:
                over_pieces([(u, 2, ()) for u in (0, 3, 1, 2)])

        def arrived(k):
            whole(RD.at[k], 32).wait_recv()

        def sent():
            for k, n in enumerate((8, 4, 32, 16, 64)):
                whole(S.at[k], n).wait_send()

        return over_pieces, wave, arrived, sent

    def w_many(n):
        if n == 64:
            return W.at[0:2]
        if n == 32:
            return W.at[0]
        if n == 16:
            return W.at[0, 0]
        return W.at[0, 0, 0 : n // 4]

    def chunk_of(e):
        return e + (e // 2) * (1 - 2 * (e % 2))

    w_over, w_wave, w_arrived, w_sent = gather(
        wS, wR, wRD, lambda e, yy, zz: W.at[chunk_of(e), yy // 2, zz, yy % 2, c], w_many
    )
    o_over, o_wave, o_arrived, o_sent = gather(
        oS, oR, oRD,
        lambda e, yy, zz: WO.at[(yy // 2) * 16 + 4 * zz + 2 * (yy % 2) + c, e],
        lambda n: WO.at[0 : n // 4],
    )

    own = [(0, 0, (0, 1, 2, 3))]
    with jax.named_scope('p02_w0a'):
        for cp in w_in:
            cp.wait()
        w_over(own, 0, 1)

    with jax.named_scope('p02_tok'):
        tok_in.wait()

    def norm(r, _):
        rows = pl.ds(pl.multiple_of(r * 16, 16), 16)
        v = X[0, rows, :].astype(jnp.float32)
        ms = jnp.mean(v * v, axis=-1, keepdims=True)
        X[0, rows, :] = (v * lax.rsqrt(ms + 1e-05) * gain[...]).astype(jnp.bfloat16)
        return 0

    with jax.named_scope('p03_norm'):
        lax.fori_loop(0, BLK // 16, norm, 0)

    def x_ref(a, o, q):
        return X.at[SLOT[o % 4], 64 * a : 64 * a + 64, q * (D // NX) : (q + 1) * (D // NX)]

    def x_piece(a, u, k, q):
        sg = 1 - 2 * a
        r = sg if k == 0 else -sg
        cp = pltpu.make_async_remote_copy(
            x_ref(a, sg * u, q), x_ref(a, sg * u - r, q),
            xss.at[a, 2 if u else k, q], xrs.at[a, (u - r * sg) % 4, q],
            device_id=at_x(r), device_id_type=MESH,
        )
        cp.start()
        return cp

    def x_recv(a, u, q):
        d = x_ref(a, (1 - 2 * a) * u, q)
        pltpu.make_async_remote_copy(
            d, d, xss.at[a, 0, q], xrs.at[a, u, q], device_id=sib, device_id_type=MESH
        ).wait_recv()

    def x_forward(a, q):
        x_recv(a, 3, q)
        return x_piece(a, 3, 0, q)

    x_own = [x_piece(a, 0, k, q) for k in (0, 1) for q in range(NX) for a in (0, 1)]

    with jax.named_scope('p04_swap'):
        wo_in.wait()
        wo_swap.wait_recv()
        t = T[...].reshape(BLK, 2048)
        for h in range(4):
            WO[p, h] = t[:, 512 * h : 512 * (h + 1)].T

    with jax.named_scope('p05_o0'):
        o_over(own, 0, 2)
    with jax.named_scope('p06_wx1'):
        w_got(1)
        w_got(3)
        w_over([(0, 0, (0, 1))], 1, 3)
        w_over([(0, 0, (2, 3))], 1, 3, False)
    with jax.named_scope('p07_wx2'):
        w_got(2)
        w_over(own, 3, 4)
    with jax.named_scope('p08_w1'):
        w_wave(1)
    with jax.named_scope('p09_w2'):
        w_wave(2)
    with jax.named_scope('p10_xf'):
        x_fwd = [x_forward(a, q) for q in range(NX) for a in (0, 1)]
    with jax.named_scope('p11_w3'):
        w_wave(3)
    with jax.named_scope('p12_w4'):
        w_wave(4)
    with jax.named_scope('p13_o1'):
        o_over(own, 2, 4)
    with jax.named_scope('p14_wdone0'):
        w_arrived(0)
    with jax.named_scope('p15_x1'):
        for q in range(NX):
            for a in (0, 1):
                x_recv(a, 1, q)

    def part(lo, hi, h, first, n0=0, n1=NW):
        m = (hi - lo) * BLK

        def step(half, _):
            col = ((x + h) % 4) * 2048 + half * 1024
            xk = X[lo:hi, :, pl.ds(pl.multiple_of(col, 1024), 1024)].reshape(m, 1024)
            wkc = W[h, half, :, :, :, :, n0:n1].reshape(1024, n1 - n0)
            d = jnp.dot(xk, wkc, preferred_element_type=jnp.float32)
            if first:
                @pl.when(half == 0)
                def _():
                    acc[0:m, n0:n1] = d

                @pl.when(half > 0)
                def _():
                    acc[0:m, n0:n1] += d
            else:
                acc[0:m, n0:n1] += d
            return 0

        lax.fori_loop(0, 2, step, 0)

    def lines(e, us, first):
        h, sg = chunk_of(e), 1 - 2 * (e % 2)
        base = ((x + h) % 4) * 2048
        xs_, ws_ = [], []

        def cols(at, n):
            at = pl.multiple_of(at, n)
            xs_.append(X[0:3, :, pl.ds(at, n)].reshape(3 * BLK, n))

        for u in us:
            if e < 2:
                yy = (y + 4 + sg * u) % 4
                ws_.append(W[h, yy // 2, :, yy % 2].reshape(512, NW))
                for zz in range(4):
                    cols(base + (yy // 2) * 1024 + zz * 256 + (yy % 2) * 128, 128)
            else:
                zz = (z + 4 + sg * u) % 4
                ws_.append(W[h, :, zz].reshape(512, NW))
                for yy in range(2):
                    cols(base + yy * 1024 + zz * 256, 256)
        d = jnp.dot(
            jnp.concatenate(xs_, axis=1), jnp.concatenate(ws_, axis=0),
            preferred_element_type=jnp.float32,
        )
        if first:
            acc[...] = d
        else:
            acc[...] += d

    kv_cps = []

    def keep_kv(s, row):
        off = SLOT.index(s)
        i = (x + off) % 4
        ref = KV.at[2 * i + yh]
        ref[...] = acc[row : row + BLK, NQ:NW].astype(jnp.bfloat16)
        cp = pltpu.make_async_remote_copy(
            ref, ref, kvs.at[off], kvr.at[off], device_id=pair, device_id_type=MESH
        )
        cp.start()
        kv_cps.append(cp)

    def keep_q(s, row):
        i = (x + SLOT.index(s)) % 4
        Q[i] = acc[row : row + BLK, 0:NQ].astype(jnp.bfloat16)

    with jax.named_scope('p16_lines03'):
        for e in range(4):
            lines(e, (0, 3), e == 0)
            w_over([(u, 1, ()) for u in (0, 3, 1, 2)], e, e + 1)
    with jax.named_scope('p17_w6'):
        w_wave(6)
    with jax.named_scope('p17b_o1'):
        o_over([(3, 0, (0, 2, 3))])
    with jax.named_scope('p18_wdone1'):
        w_arrived(1)
    with jax.named_scope('p19_lines12'):
        for e in range(4):
            lines(e, (1, 2), False)
        for s in range(3):
            keep_kv(s, s * BLK)
            keep_q(s, s * BLK)
    with jax.named_scope('p21_proj1'):
        for q in range(NX):
            for a in (0, 1):
                x_recv(a, 2, q)
            h = (q - x + 4) % 4
            if q < NX - 1:
                part(3, 4, h, q == 0)
            else:
                part(3, 4, h, False, NQ, NW)
                keep_kv(3, 0)
                part(3, 4, h, False, 0, NQ)
                keep_q(3, 0)
    with jax.named_scope('p21b_o2'):
        o_over([(1, 0, (2, 3))])
    with jax.named_scope('p22_kv'):
        for off in range(4):
            i = (x + off) % 4
            ref = KV.at[2 * i + 1 - yh]
            pltpu.make_async_remote_copy(
                ref, ref, kvs.at[off], kvr.at[off], device_id=pair, device_id_type=MESH
            ).wait_recv()
    scale = HD ** (-0.5)

    def h_ref(j, a, u):
        sg = 1 - 2 * a
        return HG.at[j, (x + 4 + sg * u) % 4, 2 * a : 2 * a + 2]

    def h_send(j, a, u, k):
        sg = 1 - 2 * a
        r = 1 if k != 1 else -1
        ref = h_ref(j, a, u)
        pltpu.make_async_remote_copy(
            ref, ref, hs.at[k], hr.at[j, a, (u - r) % 4],
            device_id=at_x(r * sg), device_id_type=MESH,
        ).start()

    def h_recv(j, a, u):
        ref = h_ref(j, a, u)
        pltpu.make_async_remote_copy(
            ref, ref, hs.at[0], hr.at[j, a, u], device_id=sib, device_id_type=MESH
        ).wait_recv()

    def attend(j):
        rows = pl.ds(pl.multiple_of(j * 32, 32), 32)
        for i in range(4):
            nk = (2 * i + 2) * BLK
            q = jnp.concatenate(
                [Q[i, rows, h * HD : (h + 1) * HD] for h in range(8)], axis=0
            )
            kk = KV[0 : 2 * i + 2, :, 0:HD].reshape(nk, HD)
            vv = KV[0 : 2 * i + 2, :, HD:NKV].reshape(nk, HD)
            s = lax.dot_general(
                q, kk, (((1,), (1,)), ((), ())), preferred_element_type=jnp.float32
            ) * scale
            qpos = (2 * i + yh) * BLK + j * 32 + lax.broadcasted_iota(
                jnp.int32, (256, nk), 0
            ) % 32
            kpos = lax.broadcasted_iota(jnp.int32, (256, nk), 1)
            s = jnp.where(qpos >= kpos, s, jnp.float32(-1e30))
            e = jnp.exp(s - jnp.max(s, axis=-1, keepdims=True))
            pr = (e * (1.0 / jnp.sum(e, axis=-1, keepdims=True))).astype(jnp.bfloat16)
            o = jnp.dot(pr, vv, preferred_element_type=jnp.float32).astype(jnp.bfloat16)
            for h in range(8):
                HG[j, x, i, :, h * HD : (h + 1) * HD] = o[h * 32 : (h + 1) * 32]
            if i % 2:
                h_send(j, i // 2, 0, 0)
                h_send(j, i // 2, 0, 1)

    def h_forward(j):
        for a in (0, 1):
            h_recv(j, a, 3)
            h_send(j, a, 3, 2)

    with jax.named_scope('p24_attend'):
        attend(0)
        o_wave(2)
        attend(1)
        o_wave(3)
        attend(2)
        h_forward(0)
        attend(3)
        h_forward(1)
    with jax.named_scope('p25_o45'):
        o_wave(4)
        o_wave(5)
        o_wave(6)
    with jax.named_scope('p26_odone'):
        o_arrived(0)
        o_arrived(1)

    def out_ref(j, xx):
        return out.at[
            pl.ds(pl.multiple_of(j * 32, 32), 32), pl.ds(pl.multiple_of(xx * NO, NO), NO)
        ]

    def tile(j, n):
        t = jnp.zeros((BLK, 512), jnp.float32)
        for kc in range(8):
            wo = jnp.concatenate(
                [WO[8 * n + 2 * e + kc // 4, kc % 4] for e in range(4)], axis=1
            )
            lhs = HG[j, kc // 2, :, :, (kc % 2) * 512 : (kc % 2) * 512 + 512].reshape(BLK, 512)
            t += jnp.dot(lhs, wo, preferred_element_type=jnp.float32)
        OB[j, :, :, pl.ds(pl.multiple_of(n * 512, 512), 512)] = t.astype(
            jnp.bfloat16
        ).reshape(4, 32, 512)

    def mix(j, _):
        with jax.named_scope('m_wait'):
            for a in (0, 1):
                h_recv(j, a, 1)
                h_recv(j, a, 2)
        lax.fori_loop(0, 2, lambda n, _: (tile(j, n), 0)[1], 0)

        @pl.when(j < 2)
        def _():
            h_forward(j + 2)

        lax.fori_loop(2, 4, lambda n, _: (tile(j, n), 0)[1], 0)
        for r in (2, 1, 3):
            pltpu.make_async_remote_copy(
                OB.at[j, (x + r) % 4], out_ref(j, x), os_.at[r], or_.at[j, 4 - r],
                device_id=at_x(r), device_id_type=MESH,
            ).start()
        pltpu.make_async_copy(OB.at[j, x], out_ref(j, x), ol).start()
        return 0

    with jax.named_scope('p27_mix'):
        lax.fori_loop(0, 4, mix, 0)

    with jax.named_scope('p28_sent'):
        for cp in xsends + x_own + x_fwd + kv_cps:
            cp.wait_send()
    wo_swap.wait_send()
    w_sent()
    o_sent()
    for k in range(3):
        pltpu.make_async_remote_copy(
            HG.at[0], HG.at[0], hs.at[k], hs.at[k], device_id=sib, device_id_type=MESH
        ).wait_send()
    for r in (1, 2, 3):
        pltpu.make_async_remote_copy(
            OB.at[0], OB.at[0], os_.at[r], os_.at[r], device_id=sib, device_id_type=MESH
        ).wait_send()
    pltpu.make_async_copy(OB.at[0], OB.at[0], ol).wait()

    def finish(j, _):
        for r in (1, 2, 3):
            d = out_ref(j, (x + r) % 4)
            pltpu.make_async_remote_copy(
                d, d, os_.at[r], or_.at[j, r], device_id=sib, device_id_type=MESH
            ).wait_recv()
        return 0

    with jax.named_scope('p29_finish'):
        lax.fori_loop(0, 4, finish, 0)


def body(tokens, norm_gain, w_query, key_weight, value_weight, w_out):
    hbm = pl.BlockSpec(memory_space=pltpu.HBM)
    vmem = pl.BlockSpec(memory_space=pltpu.VMEM)
    bf = jnp.bfloat16
    dma = pltpu.SemaphoreType.DMA
    branch = pl.pallas_call(
        kernel,
        out_shape=jax.ShapeDtypeStruct((BLK, D), bf),
        in_specs=[hbm, vmem, hbm, hbm, hbm, hbm],
        out_specs=hbm,
        scratch_shapes=[
            pltpu.VMEM((4, 2, 4, 2, 2, 64, NW), bf),
            pltpu.VMEM((32, 4, 512, BLK), bf),
            pltpu.VMEM((4, BLK, D), bf),
            pltpu.VMEM((4, BLK, NQ), bf),
            pltpu.VMEM((8, BLK, NKV), bf),
            pltpu.VMEM((4, 4, 4, 32, NQ), bf),
            pltpu.VMEM((4, 4, 32, NO), bf),
            pltpu.VMEM((3 * BLK, NW), jnp.float32),
            pltpu.VMEM((2, 64, 2048), bf),
            dma((10,)), dma((4, 6)), dma((4, 6)), dma((2, 3, NX)), dma((2, 4, NX)),
            dma((5,)), dma((4, 4, 4)), dma((2,)),
            dma((5,)), dma((4, 4, 4)), dma((2,)),
            dma((4,)), dma((4,)), dma((3,)), dma((4, 2, 4)),
            dma((4,)), dma((4, 4)), dma(()),
        ],
        compiler_params=pltpu.CompilerParams(
            collective_id=0, has_side_effects=True, vmem_limit_bytes=67043328
        ),
        name="sublayer",
    )(tokens[0], norm_gain.reshape(1, D), w_query, key_weight, value_weight, w_out.T)
    return tokens.astype(jnp.float32) + branch[None].astype(jnp.float32)


def solution(mesh):
    placed = (
        P("fsdp", "seq", None),
        P(),
        P(("seq", "fsdp"), None),
        P(("seq", "fsdp"), None),
        P(("seq", "fsdp"), None),
        P(None, ("seq", "fsdp")),
    )
    return jax.shard_map(
        body, mesh=mesh, in_specs=placed, out_specs=P("fsdp", "seq", None), check_vma=False
    )
```

time: 185 us -> 155 us (0.84)
  Pallas kernels: 180 us -> 150 us
    pallas_call x1, Pallas kernels: 180 us -> 150 us  [body(): pl.pallas_call(kernel, out_shape=jax.ShapeDtypeStruct((BLK, D), bf), in_s...]
where the time goes in v2:
time: 155 us; the launch traced here: 154 us
  Pallas kernels  150 us (97%)
  other arithmetic  4.76 us (3%)
    pallas_call x1, Pallas kernels, body(): pl.pallas_call(kernel, out_shape=jax.ShapeDtypeStruct((BLK, D), bf), in_s...  150 us
    add x1, other arithmetic, body(): return tokens.astype(jnp.float32) + branch[None].astype(jnp.float32)  4.76 us

profile of v2, /device:TPU:1, one launch (start us, length us, event | category | flops | bytes accessed | tf_op | source)
XLA Modules:
  0.0 154.4 jit_solution(8737307275979169635)
XLA Ops:
  0.0 149.6 %sublayer.1 = bf16[128,8192]{1,0:T(8,128)(2,1)} custom-call(bf16[128,8192]{1,0:T(8,128)(2,1)} %bitcast.6, f32[1,8192]{1,0:T(1,128)} %bitcast.8, bf16[64,4096]{1,0:T(8,128)(2,1)} %wq.1, bf16[64,512]{1,0:T(8,128)(2,1)} %wk.1, bf16[64,512]{1,0:T(8,128)(2,1)} %wv.1, bf16[64,4096]{1,0:T(8,128)(2,1)} %bitcast.7), custom_call_target="tpu_custom_call" | custom-call | tf_op jit(solution)/shard_map/sublayer/pallas_call | solution.py:515
  149.6 4.8 %convert_add_fusion = f32[1,128,8192]{2,1,0:T(8,128)} fusion(bf16[1,128,8192]{2,1,0:T(8,128)(2,1)} %param.6, bf16[128,8192]{1,0:T(8,128)(2,1)} %sublayer.1), kind=kLoop, calls=%fused_computation | loop fusion | flops 3145728 | bytes 8388608 | tf_op jit(solution)/shard_map/add | solution.py:541

commit v3 on v2

v3 whole, which is shorter than its diff:
```python
import jax
import jax.numpy as jnp
from jax import lax
from jax.experimental import pallas as pl
from jax.experimental.pallas import tpu as pltpu
from jax.sharding import PartitionSpec as P

HD = 128
BLK = 128
D = 8192
NQ = 1024
NKV = 256
NW = NQ + NKV
NO = 2048
MESH = pl.DeviceIdType.MESH
SLOT = (0, 1, 3, 2)
NH = 640


def kernel(
    tok, gain, wq, wk, wv, wot, out,
    W, WO, XN, X, Q, KV, HG, OB, acc,
    T, PB, RB, loc, xs, xr, xss, xrs, pbs, rbr, wS, wR, wRD, oS, oR, oRD, kvs, kvr, hs, hr, os_, or_, ol,
):
    sx = lax.axis_index("seq")
    f = lax.axis_index("fsdp")
    x, yh = sx // 2, sx % 2
    z, yl, c = f // 4, (f // 2) % 2, f % 2
    y = 2 * yh + yl
    p = yh * 16 + f

    def dev(xx, yy, zz, cc):
        return (2 * xx + yy // 2, 4 * zz + 2 * (yy % 2) + cc)

    def at_x(r):
        return dev((x + r) % 4, y, z, c)

    sib = dev(x, y, z, 1 - c)
    pair = dev(x, (y + 2) % 4, z, c)

    barrier = pltpu.get_barrier_semaphore()
    peers = [at_x(1), at_x(2), at_x(3), sib, pair]
    peers += [dev(x, (y + 1) % 4, z, c), dev(x, (y + 3) % 4, z, c)]
    peers += [dev(x, y, (z + 1) % 4, c), dev(x, y, (z + 3) % 4, c)]
    for d in peers:
        pl.semaphore_signal(barrier, inc=1, device_id=d, device_id_type=MESH)

    def w_parts(t, h, make):
        def dst(g, s, lo, hi):
            return W.at[g, h, s, yh, z, yl, c, :, lo:hi]

        def wide(n, half):
            return wq.at[:, pl.ds(pl.multiple_of(n * NQ + half * 512, 512), 512)]

        def narrow(w, n):
            return w.at[:, pl.ds(pl.multiple_of(n * HD, HD), HD)]

        rem, own = [], []
        for m, d in ((0, 1), (1, 3)):
            n = (t + d) % 4
            rem.append((None, make(wide(n, t // 2), dst(0, m, 0, 512), 2 * m)))
            rem.append(
                (
                    t // 2,
                    make(narrow(wk, n), dst(0, m, 512, NH), 2 * m + 1),
                    make(narrow(wv, n), dst(0, m, 512, NH), 2 * m + 1),
                )
            )
        for s, w in ((0, wk), (1, wv)):
            own.append((None, make(wide(t, s), dst(1, s, 0, 512), 4 + 2 * s)))
            own.append((None, make(narrow(w, t), dst(1, s, 512, NH), 5 + 2 * s)))
        return rem, own

    def begin(part):
        if part[0] is None:
            part[1].start()
        else:
            for k in (0, 1):
                pl.when(part[0] == k)(part[1 + k].start)

    def local(s, d, k):
        return pltpu.make_async_copy(s, d, loc.at[4 + k])

    def remote(s, d, k):
        return pltpu.make_async_remote_copy(
            s, d, xs.at[k], xr.at[k], device_id=at_x(2), device_id_type=MESH
        )

    in_rem, in_own = w_parts(x, 0, local)
    for part in in_rem + in_own:
        begin(part)
    khalf = pl.ds(pl.multiple_of(c * 2048, 2048), 2048)
    other = pl.ds(pl.multiple_of((1 - c) * 2048, 2048), 2048)
    tok_in = pltpu.make_async_copy(tok, XN, loc.at[0])
    tok_in.start()
    wo_in = pltpu.make_async_copy(wot.at[:, khalf], T.at[c], loc.at[1])
    wo_in.start()

    with jax.named_scope('p01_barrier'):
        pl.semaphore_wait(barrier, len(peers))

    out_rem, out_own = w_parts((x + 2) % 4, 1, remote)
    for part in out_rem + out_own:
        begin(part)
    wo_swap = pltpu.make_async_remote_copy(
        wot.at[:, other], T.at[c], loc.at[2], loc.at[3], device_id=sib, device_id_type=MESH
    )
    wo_swap.start()

    got_rem, got_own = w_parts(x, 1, remote)

    def gather(S, R, RD, piece, many):
        def coords(h, a1, a2):
            g, sg = h // 2, 1 - 2 * (h % 2)
            yy = (y + 4 + sg * (a1 * g + a2 * (1 - g))) % 4
            zz = (z + 4 + sg * (a1 * (1 - g) + a2 * g)) % 4
            return yy, zz

        def ref(h, u1, u2):
            yy, zz = coords(h, u1, u2)
            return piece(h, yy, zz)

        def send(h, u1, u2, k):
            a1, a2 = ((1, 0), (-1, 0), (0, 1), (0, -1))[k]
            yy, zz = coords(h, a1, a2)
            r = ref(h, u1, u2)
            pltpu.make_async_remote_copy(
                r, r, S.at[k], R.at[h, (u1 - a1) % 4, (u2 - a2) % 4],
                device_id=dev(x, yy, zz, c), device_id_type=MESH,
            ).start()

        def across(h, u1, u2):
            r = ref(h, u1, u2)
            pltpu.make_async_remote_copy(
                r, r, S.at[4], RD.at[int(u2 == 2)], device_id=sib, device_id_type=MESH
            ).start()

        def recv(h, u1, u2):
            r = ref(h, u1, u2)
            pltpu.make_async_remote_copy(
                r, r, S.at[4], R.at[h, u1, u2], device_id=sib, device_id_type=MESH
            ).wait_recv()

        def over_pieces(steps, first=0, last=4, again=False):
            def one(h, _):
                for u1, u2, ks in steps:
                    if not again and (u1, u2) != (0, 0):
                        recv(h, u1, u2)
                    for k in ks:
                        send(h, u1, u2, k)
                    if not again:
                        across(h, u1, u2)
                return 0

            lax.fori_loop(first, last, one, 0)

        def whole(sem, n):
            return pltpu.make_async_remote_copy(
                many(n), many(n), sem, sem, device_id=sib, device_id_type=MESH
            )

        def wave(n):
            if n == 1:
                over_pieces([(3, 0, (0,))])
                over_pieces([(3, 0, (2, 3))], again=True)
                over_pieces([(1, 0, (2, 3))])
            elif n == 2:
                over_pieces([(2, 0, (2, 3)), (0, 3, (2,))])
            elif n == 3:
                over_pieces([(3, 3, (2,)), (1, 3, (2,))])
            elif n == 4:
                over_pieces([(2, 3, (2,))])
            elif n == 5:
                over_pieces([(u, 1, ()) for u in (0, 3, 1, 2)])
            elif n == 6:
                over_pieces([(u, 2, ()) for u in (0, 3, 1, 2)])

        def arrived(k):
            whole(RD.at[k], (48, 16)[k]).wait_recv()

        def sent():
            for k, n in enumerate((8, 4, 32, 16, 64)):
                whole(S.at[k], n).wait_send()

        return over_pieces, wave, arrived, sent

    def w_many(n):
        if n == 64:
            return W.at[0, 0]
        if n == 48:
            return W.at[0, 0, :, :, 0:3]
        if n == 32:
            return W.at[0, 0, 0]
        if n == 16:
            return W.at[0, 0, 0, 0]
        return W.at[0, 0, 0, 0, 0 : n // 4]

    def w_gather(g):
        return gather(
            wS.at[g], wR.at[g], wRD.at[g],
            lambda e, yy, zz: W.at[g, e % 2, e // 2, yy // 2, zz, yy % 2, c],
            w_many,
        )

    r_over, r_wave, r_arrived, r_sent = w_gather(0)
    w_over, w_wave, w_arrived, w_sent = w_gather(1)
    o_over, o_wave, o_arrived, o_sent = gather(
        oS, oR, oRD,
        lambda e, yy, zz: WO.at[(yy // 2) * 16 + 4 * zz + 2 * (yy % 2) + c, e],
        lambda n: WO.at[0 : n // 4],
    )

    own = [(0, 0, (0, 1, 2, 3))]

    def each(over, steps, pieces):
        for e in pieces:
            over(steps, e, e + 1)

    with jax.named_scope('p02_r0a'):
        for part in in_rem:
            part[1].wait()
        each(r_over, own, (0, 2))

    with jax.named_scope('p02_tok'):
        tok_in.wait()

    def norm(r, _):
        rows = pl.ds(pl.multiple_of(r * 16, 16), 16)
        v = XN[rows, :].astype(jnp.float32)
        ms = jnp.mean(v * v, axis=-1, keepdims=True)
        XN[rows, :] = (v * lax.rsqrt(ms + 1e-05) * gain[...]).astype(jnp.bfloat16)
        return 0

    with jax.named_scope('p03_norm'):
        lax.fori_loop(0, BLK // 16, norm, 0)

    def x_cols(ch):
        return pl.ds(pl.multiple_of((ch % 4) * 2048, 2048), 2048)

    def x_copy(r, h):
        o = (4 - r) % 4
        return pltpu.make_async_remote_copy(
            XN.at[:, x_cols(x + r + 2 * h)], X.at[h, SLOT[o]], xss.at[r, h], xrs.at[o, h],
            device_id=at_x(r), device_id_type=MESH,
        )

    def x_recv(o, h):
        d = X.at[h, SLOT[o]]
        pltpu.make_async_remote_copy(
            d, d, xss.at[0, 0], xrs.at[o, h], device_id=sib, device_id_type=MESH
        ).wait_recv()

    x_sends = [x_copy(r, h) for rs in ((1, 3), (2,)) for h in (0, 1) for r in rs]
    for cp in x_sends:
        cp.start()
    for h in (0, 1):
        X[h, 0] = XN[:, x_cols(x + 2 * h)]

    with jax.named_scope('p04_swap'):
        wo_in.wait()
        wo_swap.wait_recv()
        t = T[...].reshape(BLK, 2048)
        for h in range(4):
            WO[p, h] = t[:, 512 * h : 512 * (h + 1)].T

    with jax.named_scope('p05_w0a'):
        for part in in_own:
            part[1].wait()
        each(w_over, own, (0, 2))
    with jax.named_scope('p06_r0b'):
        for part in got_rem:
            part[1].wait_recv()
        each(r_over, own, (1, 3))
    with jax.named_scope('p07_r1'):
        r_wave(1)
    with jax.named_scope('p08_w0b'):
        for part in got_own:
            part[1].wait_recv()
        each(w_over, own, (1, 3))
    with jax.named_scope('p09_r2'):
        r_wave(2)
    with jax.named_scope('p10_r3'):
        r_wave(3)
    with jax.named_scope('p11_r4'):
        r_wave(4)
    with jax.named_scope('p12_w1'):
        w_wave(1)
    with jax.named_scope('p13_r56'):
        r_wave(5)
        r_wave(6)
    with jax.named_scope('p14_w2'):
        w_wave(2)
    with jax.named_scope('p14_w3'):
        w_wave(3)
    with jax.named_scope('p15_rdone'):
        r_arrived(0)
        r_arrived(1)
    with jax.named_scope('p15_x1'):
        for o in (1, 3):
            for h in (0, 1):
                x_recv(o, h)

    def product(g, lo, hi, n0, n1, step):
        h, k = step // 2, step % 2
        wkc = jnp.concatenate(
            [W[g, h, t, k, :, :, :, :, n0:n1].reshape(1024, n1 - n0) for t in (0, 1)], axis=1
        )
        return jnp.dot(
            X[h, lo:hi, :, k * 1024 : (k + 1) * 1024].reshape((hi - lo) * BLK, 1024), wkc,
            preferred_element_type=jnp.float32,
        )

    def add_up(g, lo, hi, n0, n1, steps=(0, 1, 2, 3)):
        rows = slice(lo * BLK, hi * BLK)
        for step in steps:
            d = product(g, lo, hi, n0, n1, step)
            for t in (0, 1):
                cols = slice(t * NH + n0, t * NH + n1)
                part = d[:, t * (n1 - n0) : (t + 1) * (n1 - n0)]
                if step == 0:
                    acc[rows, cols] = part
                else:
                    acc[rows, cols] += part

    pb_cps = []

    def pb_send(s, n0, n1):
        i = (x + SLOT.index(s)) % 4
        for m, r in ((0, 1), (1, 3)):
            PB[s, m, :, n0:n1] = acc[
                s * BLK : (s + 1) * BLK, m * NH + n0 : m * NH + n1
            ].astype(jnp.bfloat16)
            cp = pltpu.make_async_remote_copy(
                PB.at[s, m, :, n0:n1], RB.at[x // 2, i, :, n0:n1],
                pbs.at[s, m, n0 // 512], rbr.at[x // 2, i, n0 // 512],
                device_id=at_x(r), device_id_type=MESH,
            )
            cp.start()
            pb_cps.append(cp)

    def rb_recv(n0, n1):
        for b in (0, 1):
            for i in range(4):
                ref = RB.at[b, i, :, n0:n1]
                pltpu.make_async_remote_copy(
                    ref, ref, pbs.at[0, 0, 0], rbr.at[b, i, n0 // 512],
                    device_id=sib, device_id_type=MESH,
                ).wait_recv()

    with jax.named_scope('p16_rem3a'):
        add_up(0, 0, 3, 0, NH, (0, 1))
    with jax.named_scope('p16_w4'):
        w_wave(4)
    with jax.named_scope('p16_rem3b'):
        add_up(0, 0, 3, 0, NH, (2, 3))
        for s in range(3):
            pb_send(s, 512, NH)
        for s in range(2):
            pb_send(s, 0, 512)
    with jax.named_scope('p16_o0'):
        o_over([(0, 0, (0, 1))], 0, 2)
        o_over(own, 2, 4)
        o_over([(0, 0, (2, 3))], 0, 1, True)
    with jax.named_scope('p16_w5'):
        w_wave(5)
    with jax.named_scope('p17_x2'):
        for h in (0, 1):
            x_recv(2, h)
    with jax.named_scope('p17_rem1'):
        add_up(0, 3, 4, 512, NH)
        pb_send(3, 512, NH)
        pb_send(2, 0, 512)
        add_up(0, 3, 4, 0, 512)
        pb_send(3, 0, 512)
    with jax.named_scope('p18_w6'):
        w_wave(6)
    with jax.named_scope('p18_wdone'):
        w_arrived(0)
        w_arrived(1)
    with jax.named_scope('p19_kv'):
        add_up(1, 0, 4, 512, NH)
    with jax.named_scope('p20_rbkv'):
        rb_recv(512, NH)

    kv_cps = []

    def total(s, b, lo, hi):
        i = (x + SLOT.index(s)) % 4
        t = acc[s * BLK : (s + 1) * BLK, b * NH + lo : b * NH + hi]
        return (t + RB[b, i, :, lo:hi].astype(jnp.float32)).astype(jnp.bfloat16)

    with jax.named_scope('p20_keepkv'):
        for s in range(4):
            off = SLOT.index(s)
            ref = KV.at[2 * ((x + off) % 4) + yh]
            ref[:, 0:HD] = total(s, 0, 512, NH)
            ref[:, HD:NKV] = total(s, 1, 512, NH)
            cp = pltpu.make_async_remote_copy(
                ref, ref, kvs.at[off], kvr.at[off], device_id=pair, device_id_type=MESH
            )
            cp.start()
            kv_cps.append(cp)
    with jax.named_scope('p20_o'):
        o_over([(3, 0, (0,))], 0, 2)
        o_over([(3, 0, (0, 2, 3)), (1, 0, (2, 3))], 2, 4)
        o_over([(0, 0, (2, 3))], 1, 2, True)
        o_over([(3, 0, (2, 3))], 0, 2, True)
        o_over([(1, 0, (2, 3))], 0, 2)
    with jax.named_scope('p21_q'):
        add_up(1, 0, 4, 0, 512)
    with jax.named_scope('p21_rbq'):
        rb_recv(0, 512)
    with jax.named_scope('p21_keepq'):
        for s in range(4):
            i = (x + SLOT.index(s)) % 4
            Q[i, :, 0:512] = total(s, 0, 0, 512)
            Q[i, :, 512:NQ] = total(s, 1, 0, 512)
    with jax.named_scope('p22_kv'):
        for off in range(4):
            i = (x + off) % 4
            ref = KV.at[2 * i + 1 - yh]
            pltpu.make_async_remote_copy(
                ref, ref, kvs.at[off], kvr.at[off], device_id=pair, device_id_type=MESH
            ).wait_recv()
    scale = HD ** (-0.5)

    def h_ref(j, a, u):
        sg = 1 - 2 * a
        return HG.at[j, (x + 4 + sg * u) % 4, 2 * a : 2 * a + 2]

    def h_send(j, a, u, k):
        sg = 1 - 2 * a
        r = 1 if k != 1 else -1
        ref = h_ref(j, a, u)
        pltpu.make_async_remote_copy(
            ref, ref, hs.at[k], hr.at[j, a, (u - r) % 4],
            device_id=at_x(r * sg), device_id_type=MESH,
        ).start()

    def h_recv(j, a, u):
        ref = h_ref(j, a, u)
        pltpu.make_async_remote_copy(
            ref, ref, hs.at[0], hr.at[j, a, u], device_id=sib, device_id_type=MESH
        ).wait_recv()

    def attend(j):
        rows = pl.ds(pl.multiple_of(j * 32, 32), 32)
        for i in range(4):
            nk = (2 * i + 2) * BLK
            q = jnp.concatenate(
                [Q[i, rows, h * HD : (h + 1) * HD] for h in range(8)], axis=0
            )
            kk = KV[0 : 2 * i + 2, :, 0:HD].reshape(nk, HD)
            vv = KV[0 : 2 * i + 2, :, HD:NKV].reshape(nk, HD)
            s = lax.dot_general(
                q, kk, (((1,), (1,)), ((), ())), preferred_element_type=jnp.float32
            ) * scale
            qpos = (2 * i + yh) * BLK + j * 32 + lax.broadcasted_iota(
                jnp.int32, (256, nk), 0
            ) % 32
            kpos = lax.broadcasted_iota(jnp.int32, (256, nk), 1)
            s = jnp.where(qpos >= kpos, s, jnp.float32(-1e30))
            e = jnp.exp(s - jnp.max(s, axis=-1, keepdims=True))
            pr = (e * (1.0 / jnp.sum(e, axis=-1, keepdims=True))).astype(jnp.bfloat16)
            o = jnp.dot(pr, vv, preferred_element_type=jnp.float32).astype(jnp.bfloat16)
            for h in range(8):
                HG[j, x, i, :, h * HD : (h + 1) * HD] = o[h * 32 : (h + 1) * 32]
            if i % 2:
                h_send(j, i // 2, 0, 0)
                h_send(j, i // 2, 0, 1)

    def h_forward(j):
        for a in (0, 1):
            h_recv(j, a, 3)
            h_send(j, a, 3, 2)

    with jax.named_scope('p24_attend0'):
        attend(0)
    with jax.named_scope('p24_o3'):
        o_over([(0, 3, (2,)), (2, 0, (2, 3)), (3, 3, (2,))], 2, 4)
    with jax.named_scope('p24_p_attend1'):
        attend(1)
    with jax.named_scope('p24b_o4'):
        o_over([(2, 0, (2, 3)), (0, 3, (2,))], 0, 2)
        o_over([(1, 3, (2,))], 2, 4)
    with jax.named_scope('p24c_attend2'):
        attend(2)
    with jax.named_scope('p24d_hf0'):
        h_forward(0)
    with jax.named_scope('p24e_attend3'):
        attend(3)
    with jax.named_scope('p24e_o5'):
        o_over([(2, 3, (2,))], 2, 4)
    with jax.named_scope('p24f_hf1'):
        h_forward(1)
    with jax.named_scope('p24g_o6'):
        o_over([(3, 3, (2,)), (1, 3, (2,))], 0, 2)
    with jax.named_scope('p24g_hf2'):
        h_forward(2)
    with jax.named_scope('p24h_o7'):
        o_over([(2, 3, (2,))], 0, 2)
    with jax.named_scope('p25_o5'):
        o_wave(5)
    with jax.named_scope('p26_odone0'):
        o_arrived(0)

    def out_ref(j, xx):
        return out.at[
            pl.ds(pl.multiple_of(j * 32, 32), 32), pl.ds(pl.multiple_of(xx * NO, NO), NO)
        ]

    order = [(0, 0), (0, 1), (0, 3), (1, 0), (1, 1), (1, 3), (3, 0), (3, 1)]
    order += [(3, 3), (0, 2), (1, 2), (3, 2), (2, 0), (2, 1), (2, 2), (2, 3)]

    def chip_at(q):
        yy, zz = (y + order[q][0]) % 4, (z + order[q][1]) % 4
        return (yy // 2) * 8 + 2 * zz + yy % 2

    def tile(j, n):
        t = jnp.zeros((BLK, 512), jnp.float32)
        for kc in range(8):
            wo = jnp.concatenate(
                [WO[2 * chip_at(4 * n + e) + kc // 4, kc % 4] for e in range(4)], axis=1
            )
            lhs = HG[j, kc // 2, :, :, (kc % 2) * 512 : (kc % 2) * 512 + 512].reshape(BLK, 512)
            t += jnp.dot(lhs, wo, preferred_element_type=jnp.float32)
        OB[j, :, :, n * 512 : (n + 1) * 512] = t.astype(jnp.bfloat16).reshape(4, 32, 512)
        for q in range(4 * n, 4 * n + 4):
            col = pl.multiple_of(x * NO + chip_at(q) * BLK, BLK)
            dst = out.at[pl.ds(pl.multiple_of(j * 32, 32), 32), pl.ds(col, BLK)]
            cols = slice(q * BLK, (q + 1) * BLK)
            for r in (2, 1, 3):
                pltpu.make_async_remote_copy(
                    OB.at[j, (x + r) % 4, :, cols], dst, os_.at[r], or_.at[j, 4 - r],
                    device_id=at_x(r), device_id_type=MESH,
                ).start()
            pltpu.make_async_copy(OB.at[j, x, :, cols], dst, ol).start()

    def early(j, _):
        with jax.named_scope('m_wait'):
            for a in (0, 1):
                h_recv(j, a, 1)
                h_recv(j, a, 2)
        tile(j, 0)
        tile(j, 1)
        return 0

    def late(j, _):
        tile(j, 2)
        tile(j, 3)
        return 0

    with jax.named_scope('p27_mix0'):
        lax.fori_loop(0, 1, early, 0)
    with jax.named_scope('p27_mix0_hf3'):
        h_forward(3)
    with jax.named_scope('p27_mix12'):
        lax.fori_loop(1, 3, early, 0)
    with jax.named_scope('p27_o6'):
        o_wave(6)
    with jax.named_scope('p27_p_mix3'):
        lax.fori_loop(3, 4, early, 0)
    with jax.named_scope('p27_q_odone1'):
        o_arrived(1)
    with jax.named_scope('p27_r_late'):
        lax.fori_loop(0, 4, late, 0)

    with jax.named_scope('p28_sent'):
        for cp in x_sends + pb_cps + kv_cps:
            cp.wait_send()
        for part in out_rem + out_own:
            part[1].wait_send()
    wo_swap.wait_send()
    r_sent()
    w_sent()
    o_sent()
    for k in range(3):
        pltpu.make_async_remote_copy(
            HG.at[0], HG.at[0], hs.at[k], hs.at[k], device_id=sib, device_id_type=MESH
        ).wait_send()
    for r in (1, 2, 3):
        pltpu.make_async_remote_copy(
            OB.at[0], OB.at[0], os_.at[r], os_.at[r], device_id=sib, device_id_type=MESH
        ).wait_send()
    pltpu.make_async_copy(OB.at[0], OB.at[0], ol).wait()

    def finish(j, _):
        for r in (1, 2, 3):
            d = out_ref(j, (x + r) % 4)
            pltpu.make_async_remote_copy(
                d, d, os_.at[r], or_.at[j, r], device_id=sib, device_id_type=MESH
            ).wait_recv()
        return 0

    with jax.named_scope('p29_finish'):
        lax.fori_loop(0, 4, finish, 0)


def body(tokens, norm_gain, w_query, key_weight, value_weight, w_out):
    hbm = pl.BlockSpec(memory_space=pltpu.HBM)
    vmem = pl.BlockSpec(memory_space=pltpu.VMEM)
    bf = jnp.bfloat16
    dma = pltpu.SemaphoreType.DMA
    branch = pl.pallas_call(
        kernel,
        out_shape=jax.ShapeDtypeStruct((BLK, D), bf),
        in_specs=[hbm, vmem, hbm, hbm, hbm, hbm],
        out_specs=hbm,
        scratch_shapes=[
            pltpu.VMEM((2, 2, 2, 2, 4, 2, 2, 64, NH), bf),
            pltpu.VMEM((32, 4, 512, BLK), bf),
            pltpu.VMEM((BLK, D), bf),
            pltpu.VMEM((2, 4, BLK, 2048), bf),
            pltpu.VMEM((4, BLK, NQ), bf),
            pltpu.VMEM((8, BLK, NKV), bf),
            pltpu.VMEM((4, 4, 4, 32, NQ), bf),
            pltpu.VMEM((4, 4, 32, NO), bf),
            pltpu.VMEM((4 * BLK, NW), jnp.float32),
            pltpu.VMEM((2, 64, 2048), bf),
            pltpu.VMEM((4, 2, BLK, NH), bf),
            pltpu.VMEM((2, 4, BLK, NH), bf),
            dma((12,)), dma((8,)), dma((8,)), dma((4, 2)), dma((4, 2)), dma((4, 2, 2)), dma((2, 4, 2)),
            dma((2, 5)), dma((2, 4, 4, 4)), dma((2, 2)),
            dma((5,)), dma((4, 4, 4)), dma((2,)),
            dma((4,)), dma((4,)), dma((3,)), dma((4, 2, 4)),
            dma((4,)), dma((4, 4)), dma(()),
        ],
        compiler_params=pltpu.CompilerParams(
            collective_id=0, has_side_effects=True, vmem_limit_bytes=60600000
        ),
        name="sublayer",
    )(tokens[0], norm_gain.reshape(1, D), w_query, key_weight, value_weight, w_out.T)
    return tokens.astype(jnp.float32) + branch[None].astype(jnp.float32)


def solution(mesh):
    placed = (
        P("fsdp", "seq", None),
        P(),
        P(("seq", "fsdp"), None),
        P(("seq", "fsdp"), None),
        P(("seq", "fsdp"), None),
        P(None, ("seq", "fsdp")),
    )
    return jax.shard_map(
        body, mesh=mesh, in_specs=placed, out_specs=P("fsdp", "seq", None), check_vma=False
    )
```

time: 155 us -> 147 us (0.948)
  Pallas kernels: 150 us -> 142 us
    pallas_call x1, Pallas kernels: 150 us -> 142 us  [body(): pl.pallas_call(kernel, out_shape=jax.ShapeDtypeStruct((BLK, D), bf), in_s...]
where the time goes in v3:
time: 147 us; the launch traced here: 146 us
  Pallas kernels  142 us (97%)
  other arithmetic  4.12 us (3%)
    pallas_call x1, Pallas kernels, body(): pl.pallas_call(kernel, out_shape=jax.ShapeDtypeStruct((BLK, D), bf), in_s...  142 us
    add x1, other arithmetic, body(): return tokens.astype(jnp.float32) + branch[None].astype(jnp.float32)  4.12 us

profile of v3, /device:TPU:1, one launch (start us, length us, event | category | flops | bytes accessed | tf_op | source)
XLA Modules:
  0.0 146.4 jit_solution(2798396058673251357)
XLA Ops:
  0.0 0.0 copy-start
  0.0 142.3 %sublayer.1 = bf16[128,8192]{1,0:T(8,128)(2,1)} custom-call(bf16[128,8192]{1,0:T(8,128)(2,1)} %bitcast.6, f32[1,8192]{1,0:T(1,128)} %bitcast.8, bf16[64,4096]{1,0:T(8,128)(2,1)} %wq.1, bf16[64,512]{1,0:T(8,128)(2,1)} %wk.1, bf16[64,512]{1,0:T(8,128)(2,1)} %wv.1, bf16[64,4096]{1,0:T(8,128)(2,1)} %bitcast.7), custom_call_target="tpu_custom_call" | custom-call | tf_op jit(solution)/shard_map/sublayer/pallas_call | solution.py:604
  142.3 0.0 copy-done
  142.3 4.1 %convert_add_fusion = f32[1,128,8192]{2,1,0:T(8,128)} fusion(bf16[1,128,8192]{2,1,0:T(8,128)(2,1)S(1)} %copy-done, bf16[128,8192]{1,0:T(8,128)(2,1)} %sublayer.1), kind=kLoop, calls=%fused_computation | loop fusion | flops 3145728 | bytes 8388608 | tf_op jit(solution)/shard_map/add | solution.py:633
Async XLA Ops:
  0.0 142.3 %copy-start = (bf16[1,128,8192]{2,1,0:T(8,128)(2,1)S(1)}, bf16[1,128,8192]{2,1,0:T(8,128)(2,1)}, u32[]{:S(2)}) copy-start(bf16[1,128,8192]{2,1,0:T(8,128)(2,1)} %param.6) | copy-start | bytes 6291460

commit v4 on v3

--- a/solution.py
+++ b/solution.py
@@ -300,24 +300,21 @@
             for h in (0, 1):
                 x_recv(o, h)
 
-    def product(g, lo, hi, n0, n1, step):
-        h, k = step // 2, step % 2
-        wkc = jnp.concatenate(
-            [W[g, h, t, k, :, :, :, :, n0:n1].reshape(1024, n1 - n0) for t in (0, 1)], axis=1
-        )
-        return jnp.dot(
-            X[h, lo:hi, :, k * 1024 : (k + 1) * 1024].reshape((hi - lo) * BLK, 1024), wkc,
-            preferred_element_type=jnp.float32,
-        )
-
-    def add_up(g, lo, hi, n0, n1, steps=(0, 1, 2, 3)):
+    def add_up(g, lo, hi, n0, n1, chunks=(0, 1)):
         rows = slice(lo * BLK, hi * BLK)
-        for step in steps:
-            d = product(g, lo, hi, n0, n1, step)
+        n = n1 - n0
+        for h in chunks:
+            wkc = jnp.concatenate(
+                [W[g, h, t, :, :, :, :, :, n0:n1].reshape(2048, n) for t in (0, 1)], axis=1
+            )
+            d = jnp.dot(
+                X[h, lo:hi].reshape((hi - lo) * BLK, 2048), wkc,
+                preferred_element_type=jnp.float32,
+            )
             for t in (0, 1):
                 cols = slice(t * NH + n0, t * NH + n1)
-                part = d[:, t * (n1 - n0) : (t + 1) * (n1 - n0)]
-                if step == 0:
+                part = d[:, t * n : (t + 1) * n]
+                if h == 0:
                     acc[rows, cols] = part
                 else:
                     acc[rows, cols] += part
@@ -348,15 +345,14 @@
                 ).wait_recv()
 
     with jax.named_scope('p16_rem3a'):
-        add_up(0, 0, 3, 0, NH, (0, 1))
+        add_up(0, 0, 3, 0, NH, (0,))
     with jax.named_scope('p16_w4'):
         w_wave(4)
     with jax.named_scope('p16_rem3b'):
-        add_up(0, 0, 3, 0, NH, (2, 3))
+        add_up(0, 0, 3, 0, NH, (1,))
         for s in range(3):
             pb_send(s, 512, NH)
-        for s in range(2):
-            pb_send(s, 0, 512)
+        pb_send(0, 0, 512)
     with jax.named_scope('p16_o0'):
         o_over([(0, 0, (0, 1))], 0, 2)
         o_over(own, 2, 4)
@@ -369,11 +365,13 @@
     with jax.named_scope('p17_rem1'):
         add_up(0, 3, 4, 512, NH)
         pb_send(3, 512, NH)
-        pb_send(2, 0, 512)
+        for s in (1, 2):
+            pb_send(s, 0, 512)
+    with jax.named_scope('p18_w6'):
+        w_wave(6)
+    with jax.named_scope('p18_rem1q'):
         add_up(0, 3, 4, 0, 512)
         pb_send(3, 0, 512)
-    with jax.named_scope('p18_w6'):
-        w_wave(6)
     with jax.named_scope('p18_wdone'):
         w_arrived(0)
         w_arrived(1)
@@ -384,44 +382,38 @@
 
     kv_cps = []
 
-    def total(s, b, lo, hi):
-        i = (x + SLOT.index(s)) % 4
-        t = acc[s * BLK : (s + 1) * BLK, b * NH + lo : b * NH + hi]
+    def total(i, b, lo, hi):
+        off = (i + 4 - x) % 4
+        slot = off + (off // 2) * (1 - 2 * (off % 2))
+        t = acc[pl.ds(pl.multiple_of(slot * BLK, BLK), BLK), b * NH + lo : b * NH + hi]
         return (t + RB[b, i, :, lo:hi].astype(jnp.float32)).astype(jnp.bfloat16)
 
     with jax.named_scope('p20_keepkv'):
-        for s in range(4):
-            off = SLOT.index(s)
-            ref = KV.at[2 * ((x + off) % 4) + yh]
-            ref[:, 0:HD] = total(s, 0, 512, NH)
-            ref[:, HD:NKV] = total(s, 1, 512, NH)
+        for i in range(4):
+            ref = KV.at[2 * i + yh]
+            ref[:, 0:HD] = total(i, 0, 512, NH)
+            ref[:, HD:NKV] = total(i, 1, 512, NH)
             cp = pltpu.make_async_remote_copy(
-                ref, ref, kvs.at[off], kvr.at[off], device_id=pair, device_id_type=MESH
+                ref, ref, kvs.at[i], kvr.at[i], device_id=pair, device_id_type=MESH
             )
             cp.start()
             kv_cps.append(cp)
     with jax.named_scope('p20_o'):
         o_over([(3, 0, (0,))], 0, 2)
-        o_over([(3, 0, (0, 2, 3)), (1, 0, (2, 3))], 2, 4)
-        o_over([(0, 0, (2, 3))], 1, 2, True)
-        o_over([(3, 0, (2, 3))], 0, 2, True)
-        o_over([(1, 0, (2, 3))], 0, 2)
+        o_over([(3, 0, (2, 3)), (1, 0, (2, 3))], 2, 4)
     with jax.named_scope('p21_q'):
         add_up(1, 0, 4, 0, 512)
     with jax.named_scope('p21_rbq'):
         rb_recv(0, 512)
     with jax.named_scope('p21_keepq'):
-        for s in range(4):
-            i = (x + SLOT.index(s)) % 4
-            Q[i, :, 0:512] = total(s, 0, 0, 512)
-            Q[i, :, 512:NQ] = total(s, 1, 0, 512)
-    with jax.named_scope('p22_kv'):
-        for off in range(4):
-            i = (x + off) % 4
-            ref = KV.at[2 * i + 1 - yh]
-            pltpu.make_async_remote_copy(
-                ref, ref, kvs.at[off], kvr.at[off], device_id=pair, device_id_type=MESH
-            ).wait_recv()
+        for i in range(4):
+            Q[i, :, 0:512] = total(i, 0, 0, 512)
+            Q[i, :, 512:NQ] = total(i, 1, 0, 512)
+    with jax.named_scope('p21_o'):
+        o_over([(3, 0, (0,))], 2, 4, True)
+        o_over([(0, 0, (2, 3))], 1, 2, True)
+        o_over([(3, 0, (2, 3))], 0, 2, True)
+        o_over([(1, 0, (2, 3))], 0, 2)
     scale = HD ** (-0.5)
 
     def h_ref(j, a, u):
@@ -447,6 +439,11 @@
         rows = pl.ds(pl.multiple_of(j * 32, 32), 32)
         for i in range(4):
             nk = (2 * i + 2) * BLK
+            if j == 0:
+                ref = KV.at[2 * i + 1 - yh]
+                pltpu.make_async_remote_copy(
+                    ref, ref, kvs.at[i], kvr.at[i], device_id=pair, device_id_type=MESH
+                ).wait_recv()
             q = jnp.concatenate(
                 [Q[i, rows, h * HD : (h + 1) * HD] for h in range(8)], axis=0
             )
@@ -476,10 +473,10 @@
 
     with jax.named_scope('p24_attend0'):
         attend(0)
-    with jax.named_scope('p24_o3'):
+    with jax.named_scope('p24_attend1'):
+        attend(1)
+    with jax.named_scope('p24a_o3'):
         o_over([(0, 3, (2,)), (2, 0, (2, 3)), (3, 3, (2,))], 2, 4)
-    with jax.named_scope('p24_p_attend1'):
-        attend(1)
     with jax.named_scope('p24b_o4'):
         o_over([(2, 0, (2, 3)), (0, 3, (2,))], 0, 2)
         o_over([(1, 3, (2,))], 2, 4)
@@ -554,16 +551,20 @@
         lax.fori_loop(0, 1, early, 0)
     with jax.named_scope('p27_mix0_hf3'):
         h_forward(3)
-    with jax.named_scope('p27_mix12'):
-        lax.fori_loop(1, 3, early, 0)
+    with jax.named_scope('p27_mix1'):
+        lax.fori_loop(1, 2, early, 0)
     with jax.named_scope('p27_o6'):
         o_wave(6)
-    with jax.named_scope('p27_p_mix3'):
-        lax.fori_loop(3, 4, early, 0)
+    with jax.named_scope('p27_p_mix2'):
+        lax.fori_loop(2, 3, early, 0)
     with jax.named_scope('p27_q_odone1'):
         o_arrived(1)
     with jax.named_scope('p27_r_late'):
-        lax.fori_loop(0, 4, late, 0)
+        lax.fori_loop(0, 2, late, 0)
+    with jax.named_scope('p27_s_mix3'):
+        lax.fori_loop(3, 4, early, 0)
+    with jax.named_scope('p27_t_late'):
+        lax.fori_loop(2, 4, late, 0)
 
     with jax.named_scope('p28_sent'):
         for cp in x_sends + pb_cps + kv_cps:

time: 147 us -> 142 us (0.966)
  Pallas kernels: 142 us -> 138 us
    pallas_call x1, Pallas kernels: 142 us -> 138 us  [body(): pl.pallas_call(kernel, out_shape=jax.ShapeDtypeStruct((BLK, D), bf), in_s...]
where the time goes in v4:
time: 142 us
  Pallas kernels  138 us (97%)
  other arithmetic  4.12 us (3%)
    pallas_call x1, Pallas kernels, body(): pl.pallas_call(kernel, out_shape=jax.ShapeDtypeStruct((BLK, D), bf), in_s...  138 us
    add x1, other arithmetic, body(): return tokens.astype(jnp.float32) + branch[None].astype(jnp.float32)  4.12 us

profile of v4, /device:TPU:1, one launch (start us, length us, event | category | flops | bytes accessed | tf_op | source)
XLA Modules:
  0.0 142.3 jit_solution(4204010941172888547)
XLA Ops:
  0.0 0.0 copy-start
  0.0 138.1 %sublayer.1 = bf16[128,8192]{1,0:T(8,128)(2,1)} custom-call(bf16[128,8192]{1,0:T(8,128)(2,1)} %bitcast.6, f32[1,8192]{1,0:T(1,128)} %bitcast.8, bf16[64,4096]{1,0:T(8,128)(2,1)} %wq.1, bf16[64,512]{1,0:T(8,128)(2,1)} %wk.1, bf16[64,512]{1,0:T(8,128)(2,1)} %wv.1, bf16[64,4096]{1,0:T(8,128)(2,1)} %bitcast.7), custom_call_target="tpu_custom_call" | custom-call | tf_op jit(solution)/shard_map/sublayer/pallas_call | solution.py:605
  138.1 0.0 copy-done
  138.1 4.1 %convert_add_fusion = f32[1,128,8192]{2,1,0:T(8,128)} fusion(bf16[1,128,8192]{2,1,0:T(8,128)(2,1)S(1)} %copy-done, bf16[128,8192]{1,0:T(8,128)(2,1)} %sublayer.1), kind=kLoop, calls=%fused_computation | loop fusion | flops 3145728 | bytes 8388608 | tf_op jit(solution)/shard_map/add | solution.py:634
Async XLA Ops:
  0.0 138.1 %copy-start = (bf16[1,128,8192]{2,1,0:T(8,128)(2,1)S(1)}, bf16[1,128,8192]{2,1,0:T(8,128)(2,1)}, u32[]{:S(2)}) copy-start(bf16[1,128,8192]{2,1,0:T(8,128)(2,1)} %param.6) | copy-start | bytes 6291460

commit v5 on v4

--- a/solution.py
+++ b/solution.py
@@ -79,11 +79,11 @@
                 pl.when(part[0] == k)(part[1 + k].start)
 
     def local(s, d, k):
-        return pltpu.make_async_copy(s, d, loc.at[4 + k])
+        return pltpu.make_async_copy(s, d, loc.at[4 + k // 4])
 
     def remote(s, d, k):
         return pltpu.make_async_remote_copy(
-            s, d, xs.at[k], xr.at[k], device_id=at_x(2), device_id_type=MESH
+            s, d, xs, xr.at[k // 4], device_id=at_x(2), device_id_type=MESH
         )
 
     in_rem, in_own = w_parts(x, 0, local)
@@ -107,7 +107,15 @@
     )
     wo_swap.start()
 
-    got_rem, got_own = w_parts(x, 1, remote)
+    def w_local(g):
+        d = W.at[g, 0, :, yh, z, yl, c]
+        pltpu.make_async_copy(d, d, loc.at[4 + g]).wait()
+
+    def w_got(g):
+        d = W.at[g, 1, :, yh, z, yl, c]
+        pltpu.make_async_remote_copy(
+            d, d, xs, xr.at[g], device_id=at_x(2), device_id_type=MESH
+        ).wait_recv()
 
     def gather(S, R, RD, piece, many):
         def coords(h, a1, a2):
@@ -120,12 +128,15 @@
             yy, zz = coords(h, u1, u2)
             return piece(h, yy, zz)
 
+        def lane(u1, u2):
+            return {0: u1 - 1, 1: 7, 2: 8, 3: 3 + u1}[u2]
+
         def send(h, u1, u2, k):
             a1, a2 = ((1, 0), (-1, 0), (0, 1), (0, -1))[k]
             yy, zz = coords(h, a1, a2)
             r = ref(h, u1, u2)
             pltpu.make_async_remote_copy(
-                r, r, S.at[k], R.at[h, (u1 - a1) % 4, (u2 - a2) % 4],
+                r, r, S.at[k], R.at[h, lane((u1 - a1) % 4, (u2 - a2) % 4)],
                 device_id=dev(x, yy, zz, c), device_id_type=MESH,
             ).start()
 
@@ -136,15 +147,15 @@
             ).start()
 
         def recv(h, u1, u2):
-            r = ref(h, u1, u2)
+            r = ref(h, u1, u2) if u2 in (0, 3) else many(4)
             pltpu.make_async_remote_copy(
-                r, r, S.at[4], R.at[h, u1, u2], device_id=sib, device_id_type=MESH
+                r, r, S.at[4], R.at[h, lane(u1, u2)], device_id=sib, device_id_type=MESH
             ).wait_recv()
 
         def over_pieces(steps, first=0, last=4, again=False):
             def one(h, _):
                 for u1, u2, ks in steps:
-                    if not again and (u1, u2) != (0, 0):
+                    if not again and (u1, u2) != (0, 0) and (u2 in (0, 3) or u1 == 0):
                         recv(h, u1, u2)
                     for k in ks:
                         send(h, u1, u2, k)
@@ -217,8 +228,7 @@
             over(steps, e, e + 1)
 
     with jax.named_scope('p02_r0a'):
-        for part in in_rem:
-            part[1].wait()
+        w_local(0)
         each(r_over, own, (0, 2))
 
     with jax.named_scope('p02_tok'):
@@ -240,15 +250,14 @@
     def x_copy(r, h):
         o = (4 - r) % 4
         return pltpu.make_async_remote_copy(
-            XN.at[:, x_cols(x + r + 2 * h)], X.at[h, SLOT[o]], xss.at[r, h], xrs.at[o, h],
+            XN.at[:, x_cols(x + r + 2 * h)], X.at[h, SLOT[o]], xss, xrs.at[int(o == 2)],
             device_id=at_x(r), device_id_type=MESH,
         )
 
-    def x_recv(o, h):
-        d = X.at[h, SLOT[o]]
-        pltpu.make_async_remote_copy(
-            d, d, xss.at[0, 0], xrs.at[o, h], device_id=sib, device_id_type=MESH
-        ).wait_recv()
+    def x_wait(d, k):
+        return pltpu.make_async_remote_copy(
+            d, d, xss, xrs.at[k], device_id=sib, device_id_type=MESH
+        )
 
     x_sends = [x_copy(r, h) for rs in ((1, 3), (2,)) for h in (0, 1) for r in rs]
     for cp in x_sends:
@@ -264,18 +273,15 @@
             WO[p, h] = t[:, 512 * h : 512 * (h + 1)].T
 
     with jax.named_scope('p05_w0a'):
-        for part in in_own:
-            part[1].wait()
+        w_local(1)
         each(w_over, own, (0, 2))
     with jax.named_scope('p06_r0b'):
-        for part in got_rem:
-            part[1].wait_recv()
+        w_got(0)
         each(r_over, own, (1, 3))
     with jax.named_scope('p07_r1'):
         r_wave(1)
     with jax.named_scope('p08_w0b'):
-        for part in got_own:
-            part[1].wait_recv()
+        w_got(1)
         each(w_over, own, (1, 3))
     with jax.named_scope('p09_r2'):
         r_wave(2)
@@ -296,9 +302,7 @@
         r_arrived(0)
         r_arrived(1)
     with jax.named_scope('p15_x1'):
-        for o in (1, 3):
-            for h in (0, 1):
-                x_recv(o, h)
+        x_wait(X.at[:, 1:3], 0).wait_recv()
 
     def add_up(g, lo, hi, n0, n1, chunks=(0, 1)):
         rows = slice(lo * BLK, hi * BLK)
@@ -318,8 +322,6 @@
                     acc[rows, cols] = part
                 else:
                     acc[rows, cols] += part
-
-    pb_cps = []
 
     def pb_send(s, n0, n1):
         i = (x + SLOT.index(s)) % 4
@@ -329,20 +331,16 @@
             ].astype(jnp.bfloat16)
             cp = pltpu.make_async_remote_copy(
                 PB.at[s, m, :, n0:n1], RB.at[x // 2, i, :, n0:n1],
-                pbs.at[s, m, n0 // 512], rbr.at[x // 2, i, n0 // 512],
+                pbs.at[n0 // 512], rbr.at[n0 // 512],
                 device_id=at_x(r), device_id_type=MESH,
             )
             cp.start()
-            pb_cps.append(cp)
-
-    def rb_recv(n0, n1):
-        for b in (0, 1):
-            for i in range(4):
-                ref = RB.at[b, i, :, n0:n1]
-                pltpu.make_async_remote_copy(
-                    ref, ref, pbs.at[0, 0, 0], rbr.at[b, i, n0 // 512],
-                    device_id=sib, device_id_type=MESH,
-                ).wait_recv()
+
+    def partial(ref, n0, n1):
+        ref = ref.at[:, :, :, n0:n1]
+        return pltpu.make_async_remote_copy(
+            ref, ref, pbs.at[n0 // 512], rbr.at[n0 // 512], device_id=sib, device_id_type=MESH
+        )
 
     with jax.named_scope('p16_rem3a'):
         add_up(0, 0, 3, 0, NH, (0,))
@@ -360,8 +358,7 @@
     with jax.named_scope('p16_w5'):
         w_wave(5)
     with jax.named_scope('p17_x2'):
-        for h in (0, 1):
-            x_recv(2, h)
+        x_wait(X.at[:, 3], 1).wait_recv()
     with jax.named_scope('p17_rem1'):
         add_up(0, 3, 4, 512, NH)
         pb_send(3, 512, NH)
@@ -378,9 +375,7 @@
     with jax.named_scope('p19_kv'):
         add_up(1, 0, 4, 512, NH)
     with jax.named_scope('p20_rbkv'):
-        rb_recv(512, NH)
-
-    kv_cps = []
+        partial(RB, 512, NH).wait_recv()
 
     def total(i, b, lo, hi):
         off = (i + 4 - x) % 4
@@ -394,17 +389,16 @@
             ref[:, 0:HD] = total(i, 0, 512, NH)
             ref[:, HD:NKV] = total(i, 1, 512, NH)
             cp = pltpu.make_async_remote_copy(
-                ref, ref, kvs.at[i], kvr.at[i], device_id=pair, device_id_type=MESH
+                ref, ref, kvs, kvr.at[i], device_id=pair, device_id_type=MESH
             )
             cp.start()
-            kv_cps.append(cp)
     with jax.named_scope('p20_o'):
         o_over([(3, 0, (0,))], 0, 2)
         o_over([(3, 0, (2, 3)), (1, 0, (2, 3))], 2, 4)
     with jax.named_scope('p21_q'):
         add_up(1, 0, 4, 0, 512)
     with jax.named_scope('p21_rbq'):
-        rb_recv(0, 512)
+        partial(RB, 0, 512).wait_recv()
     with jax.named_scope('p21_keepq'):
         for i in range(4):
             Q[i, :, 0:512] = total(i, 0, 0, 512)
@@ -425,14 +419,13 @@
         r = 1 if k != 1 else -1
         ref = h_ref(j, a, u)
         pltpu.make_async_remote_copy(
-            ref, ref, hs.at[k], hr.at[j, a, (u - r) % 4],
+            ref, ref, hs.at[k], hr.at[j, a if (u - r) % 4 == 3 else 2],
             device_id=at_x(r * sg), device_id_type=MESH,
         ).start()
 
-    def h_recv(j, a, u):
-        ref = h_ref(j, a, u)
+    def h_wait(ref, j, k):
         pltpu.make_async_remote_copy(
-            ref, ref, hs.at[0], hr.at[j, a, u], device_id=sib, device_id_type=MESH
+            ref, ref, hs.at[0], hr.at[j, k], device_id=sib, device_id_type=MESH
         ).wait_recv()
 
     def attend(j):
@@ -442,7 +435,7 @@
             if j == 0:
                 ref = KV.at[2 * i + 1 - yh]
                 pltpu.make_async_remote_copy(
-                    ref, ref, kvs.at[i], kvr.at[i], device_id=pair, device_id_type=MESH
+                    ref, ref, kvs, kvr.at[i], device_id=pair, device_id_type=MESH
                 ).wait_recv()
             q = jnp.concatenate(
                 [Q[i, rows, h * HD : (h + 1) * HD] for h in range(8)], axis=0
@@ -468,22 +461,22 @@
 
     def h_forward(j):
         for a in (0, 1):
-            h_recv(j, a, 3)
+            h_wait(h_ref(j, a, 3), j, a)
             h_send(j, a, 3, 2)
 
     with jax.named_scope('p24_attend0'):
         attend(0)
     with jax.named_scope('p24_attend1'):
         attend(1)
+    with jax.named_scope('p24_attend2'):
+        attend(2)
     with jax.named_scope('p24a_o3'):
         o_over([(0, 3, (2,)), (2, 0, (2, 3)), (3, 3, (2,))], 2, 4)
-    with jax.named_scope('p24b_o4'):
+    with jax.named_scope('p24d_hf0'):
+        h_forward(0)
+    with jax.named_scope('p24d_o4'):
         o_over([(2, 0, (2, 3)), (0, 3, (2,))], 0, 2)
         o_over([(1, 3, (2,))], 2, 4)
-    with jax.named_scope('p24c_attend2'):
-        attend(2)
-    with jax.named_scope('p24d_hf0'):
-        h_forward(0)
     with jax.named_scope('p24e_attend3'):
         attend(3)
     with jax.named_scope('p24e_o5'):
@@ -528,16 +521,14 @@
             cols = slice(q * BLK, (q + 1) * BLK)
             for r in (2, 1, 3):
                 pltpu.make_async_remote_copy(
-                    OB.at[j, (x + r) % 4, :, cols], dst, os_.at[r], or_.at[j, 4 - r],
+                    OB.at[j, (x + r) % 4, :, cols], dst, os_.at[r - 1], or_.at[3 - r],
                     device_id=at_x(r), device_id_type=MESH,
                 ).start()
             pltpu.make_async_copy(OB.at[j, x, :, cols], dst, ol).start()
 
     def early(j, _):
         with jax.named_scope('m_wait'):
-            for a in (0, 1):
-                h_recv(j, a, 1)
-                h_recv(j, a, 2)
+            h_wait(HG.at[j, 0:2], j, 2)
         tile(j, 0)
         tile(j, 1)
         return 0
@@ -567,34 +558,32 @@
         lax.fori_loop(2, 4, late, 0)
 
     with jax.named_scope('p28_sent'):
-        for cp in x_sends + pb_cps + kv_cps:
-            cp.wait_send()
-        for part in out_rem + out_own:
-            part[1].wait_send()
-    wo_swap.wait_send()
-    r_sent()
-    w_sent()
-    o_sent()
-    for k in range(3):
+        x_wait(X.at[:, 0:3], 0).wait_send()
+        for n0, n1 in ((512, NH), (0, 512)):
+            partial(PB, n0, n1).wait_send()
+        d = KV.at[0:4]
         pltpu.make_async_remote_copy(
-            HG.at[0], HG.at[0], hs.at[k], hs.at[k], device_id=sib, device_id_type=MESH
+            d, d, kvs, kvr.at[0], device_id=pair, device_id_type=MESH
         ).wait_send()
-    for r in (1, 2, 3):
+        d = W.at[:, 0, :, 0, 0, 0, 0]
         pltpu.make_async_remote_copy(
-            OB.at[0], OB.at[0], os_.at[r], os_.at[r], device_id=sib, device_id_type=MESH
+            d, d, xs, xr.at[0], device_id=at_x(2), device_id_type=MESH
         ).wait_send()
-    pltpu.make_async_copy(OB.at[0], OB.at[0], ol).wait()
-
-    def finish(j, _):
+        wo_swap.wait_send()
+        r_sent()
+        w_sent()
+        o_sent()
+        for k in range(3):
+            pltpu.make_async_remote_copy(
+                HG.at[0], HG.at[0], hs.at[k], hr.at[0, 0], device_id=sib, device_id_type=MESH
+            ).wait_send()
+    with jax.named_scope('p29_finish'):
         for r in (1, 2, 3):
-            d = out_ref(j, (x + r) % 4)
             pltpu.make_async_remote_copy(
-                d, d, os_.at[r], or_.at[j, r], device_id=sib, device_id_type=MESH
-            ).wait_recv()
-        return 0
-
-    with jax.named_scope('p29_finish'):
-        lax.fori_loop(0, 4, finish, 0)
+                OB.at[0], OB.at[0], os_.at[r - 1], or_.at[r - 1],
+                device_id=sib, device_id_type=MESH,
+            ).wait()
+        pltpu.make_async_copy(OB.at[0], OB.at[0], ol).wait()
 
 
 def body(tokens, norm_gain, w_query, key_weight, value_weight, w_out):
@@ -620,11 +609,11 @@
             pltpu.VMEM((2, 64, 2048), bf),
             pltpu.VMEM((4, 2, BLK, NH), bf),
             pltpu.VMEM((2, 4, BLK, NH), bf),
-            dma((12,)), dma((8,)), dma((8,)), dma((4, 2)), dma((4, 2)), dma((4, 2, 2)), dma((2, 4, 2)),
-            dma((2, 5)), dma((2, 4, 4, 4)), dma((2, 2)),
-            dma((5,)), dma((4, 4, 4)), dma((2,)),
-            dma((4,)), dma((4,)), dma((3,)), dma((4, 2, 4)),
-            dma((4,)), dma((4, 4)), dma(()),
+            dma((6,)), dma(()), dma((2,)), dma(()), dma((2,)), dma((2,)), dma((2,)),
+            dma((2, 5)), dma((2, 4, 9)), dma((2, 2)),
+            dma((5,)), dma((4, 9)), dma((2,)),
+            dma(()), dma((4,)), dma((3,)), dma((4, 3)),
+            dma((3,)), dma((3,)), dma(()),
         ],
         compiler_params=pltpu.CompilerParams(
             collective_id=0, has_side_effects=True, vmem_limit_bytes=60600000

time: 142 us -> 141 us (level)
  no operation moved by 1% of the time
where the time goes in v5:
time: 141 us
  Pallas kernels  137 us (97%)
  other arithmetic  4.12 us (3%)
    pallas_call x1, Pallas kernels, body(): pl.pallas_call(kernel, out_shape=jax.ShapeDtypeStruct((BLK, D), bf), in_s...  137 us
    add x1, other arithmetic, body(): return tokens.astype(jnp.float32) + branch[None].astype(jnp.float32)  4.12 us

profile of v5, /device:TPU:1, one launch (start us, length us, event | category | flops | bytes accessed | tf_op | source)
XLA Modules:
  0.0 141.0 jit_solution(17073614597200308017)
XLA Ops:
  0.0 0.0 copy-start
  0.0 136.8 %sublayer.1 = bf16[128,8192]{1,0:T(8,128)(2,1)} custom-call(bf16[128,8192]{1,0:T(8,128)(2,1)} %bitcast.6, f32[1,8192]{1,0:T(1,128)} %bitcast.8, bf16[64,4096]{1,0:T(8,128)(2,1)} %wq.1, bf16[64,512]{1,0:T(8,128)(2,1)} %wk.1, bf16[64,512]{1,0:T(8,128)(2,1)} %wv.1, bf16[64,4096]{1,0:T(8,128)(2,1)} %bitcast.7), custom_call_target="tpu_custom_call" | custom-call | tf_op jit(solution)/shard_map/sublayer/pallas_call | solution.py:594
  136.8 0.0 copy-done
  136.8 4.1 %convert_add_fusion = f32[1,128,8192]{2,1,0:T(8,128)} fusion(bf16[1,128,8192]{2,1,0:T(8,128)(2,1)S(1)} %copy-done, bf16[128,8192]{1,0:T(8,128)(2,1)} %sublayer.1), kind=kLoop, calls=%fused_computation | loop fusion | flops 3145728 | bytes 8388608 | tf_op jit(solution)/shard_map/add | solution.py:623
Async XLA Ops:
  0.0 136.8 %copy-start = (bf16[1,128,8192]{2,1,0:T(8,128)(2,1)S(1)}, bf16[1,128,8192]{2,1,0:T(8,128)(2,1)}, u32[]{:S(2)}) copy-start(bf16[1,128,8192]{2,1,0:T(8,128)(2,1)} %param.6) | copy-start | bytes 6291460

commit v6 on v5

--- a/solution.py
+++ b/solution.py
@@ -586,6 +586,28 @@
         pltpu.make_async_copy(OB.at[0], OB.at[0], ol).wait()
 
 
+def add_rows(tok, branch, out, a, b, o, ins, outs):
+    loads = [
+        [
+            pltpu.make_async_copy(src.at[16 * k : 16 * k + 16], dst.at[k], ins.at[t, k])
+            for t, (src, dst) in enumerate(((branch, b), (tok, a)))
+        ]
+        for k in range(8)
+    ]
+    for pair in loads:
+        for cp in pair:
+            cp.start()
+    stores = []
+    for k in range(8):
+        for cp in loads[k]:
+            cp.wait()
+        o[k] = a[k].astype(jnp.float32) + b[k].astype(jnp.float32)
+        stores.append(pltpu.make_async_copy(o.at[k], out.at[16 * k : 16 * k + 16], outs.at[k]))
+        stores[-1].start()
+    for cp in stores:
+        cp.wait()
+
+
 def body(tokens, norm_gain, w_query, key_weight, value_weight, w_out):
     hbm = pl.BlockSpec(memory_space=pltpu.HBM)
     vmem = pl.BlockSpec(memory_space=pltpu.VMEM)
@@ -620,7 +642,22 @@
         ),
         name="sublayer",
     )(tokens[0], norm_gain.reshape(1, D), w_query, key_weight, value_weight, w_out.T)
-    return tokens.astype(jnp.float32) + branch[None].astype(jnp.float32)
+    total = pl.pallas_call(
+        add_rows,
+        out_shape=jax.ShapeDtypeStruct((BLK, D), jnp.float32),
+        in_specs=[hbm, hbm],
+        out_specs=hbm,
+        scratch_shapes=[
+            pltpu.VMEM((8, 16, D), bf),
+            pltpu.VMEM((8, 16, D), bf),
+            pltpu.VMEM((8, 16, D), jnp.float32),
+            dma((2, 8)),
+            dma((8,)),
+        ],
+        compiler_params=pltpu.CompilerParams(vmem_limit_bytes=64400000),
+        name="add_rows",
+    )(tokens[0], branch)
+    return total[None]
 
 
 def solution(mesh):

time: 141 us -> 141 us (level)
  other arithmetic: 4.12 us -> 0 us
  Pallas kernels: 137 us -> 140 us
    add x1 -> x0, other arithmetic: 4.12 us -> none  [body(): return tokens.astype(jnp.float32) + branch[None].astype(jnp.float32)]
    pallas_call x0 -> x1, Pallas kernels: none -> 3.59 us  [body(): pl.pallas_call(add_rows, out_shape=jax.ShapeDtypeStruct((BLK, D), jnp.flo...]
where the time goes in v6:
time: 141 us; the launch traced here: 140 us
  Pallas kernels  140 us (99%)
    pallas_call x1, Pallas kernels, body(): pl.pallas_call(kernel, out_shape=jax.ShapeDtypeStruct((BLK, D), bf), in_s...  137 us
    pallas_call x1, Pallas kernels, body(): pl.pallas_call(add_rows, out_shape=jax.ShapeDtypeStruct((BLK, D), jnp.flo...  3.59 us

profile of v6, /device:TPU:1, one launch (start us, length us, event | category | flops | bytes accessed | tf_op | source)
XLA Modules:
  0.0 140.5 jit_solution(6166974697897988571)
XLA Ops:
  0.0 136.7 %sublayer.1.branch = bf16[128,8192]{1,0:T(8,128)(2,1)} custom-call(bf16[128,8192]{1,0:T(8,128)(2,1)} %bitcast.4, f32[1,8192]{1,0:T(1,128)} %bitcast.7, bf16[64,4096]{1,0:T(8,128)(2,1)} %wq.1, bf16[64,512]{1,0:T(8,128)(2,1)} %wk.1, bf16[64,512]{1,0:T(8,128)(2,1)} %wv.1, bf16[64,4096]{1,0:T(8,128)(2,1)} %bitcast.6), custom_call_target="tpu_custom_call" | custom-call | tf_op jit(solution)/shard_map/sublayer/pallas_call | solution.py:616
  136.7 3.6 %add_rows.1 = f32[128,8192]{1,0:T(8,128)} custom-call(bf16[128,8192]{1,0:T(8,128)(2,1)} %bitcast.5, bf16[128,8192]{1,0:T(8,128)(2,1)} %sublayer.1.branch), custom_call_target="tpu_custom_call" | custom-call | tf_op jit(solution)/shard_map/add_rows/pallas_call | solution.py:645
